TPU v7x, 32 devices: a whole 2x2x4 slice. The times are simulated.
32 devices in a mesh: gx: 2 (over y), gy: 4 (over z), gz: 4 (over x, core).
Axes of the slice: x: 2, y: 2, z: 4, core: 2. Of those that a mesh axis runs over, the one named last changes fastest.
Arguments:
- forcing: float32 [3, 16, 64, 512], P(None, 'gx', 'gy', 'gz'), may hold values from -8 to 8
- viscosity: float32 [16, 64, 512], P('gx', 'gy', 'gz'), may hold values from 0.001 to 1000
Outputs:
- solution: float32 [3, 16, 64, 512], P(None, 'gx', 'gy', 'gz')
- residual: float32 [3, 16, 64, 512], P(None, 'gx', 'gy', 'gz')
All inputs are finite; a program needn't handle non-finite values.
Results may differ from a plain program's by a relative error of at most 0.00017.
Values sent between devices are 32-bit elements; how exact they have to be, the bound alone decides.
No kernel may reach another device: no remote copies, remote signals or barrier semaphores. Data moves between devices by JAX's collectives and lax.ppermute only.
A program may use at most 64 MiB of HBM per device.

v0:
```python
import jax
import jax.numpy as jnp
from jax import lax
from jax.sharding import PartitionSpec as P

ITERS = 3
CSWEEPS = 4


reaction = 1.0
relaxation = 2.0 / 3.0
neighbours = ((1, 0, 0), (-1, 0, 0), (0, 1, 0), (0, -1, 0), (0, 0, 1), (0, 0, -1))


def with_halo(x, sides, width):
    for axis, dim in sides:
        count, length = (lax.axis_size(axis), x.shape[dim])
        up = [(i, (i + 1) % count) for i in range(count - 1)]
        down = [(j, i) for i, j in up]
        last = lax.slice_in_dim(x, length - width, length, axis=dim)
        initial = lax.slice_in_dim(x, 0, width, axis=dim)
        before = lax.ppermute(last, axis, up)
        after = lax.ppermute(initial, axis, down)
        x = jnp.concatenate([before, x, after], axis=dim)
    return x


def window(padded, offset, extent):
    return padded[
        ...,
        1 + offset[0] : 1 + offset[0] + extent[0],
        1 + offset[1] : 1 + offset[1] + extent[1],
        1 + offset[2] : 1 + offset[2] + extent[2],
    ]


def viscous(values, padded_values, viscosity, padded_visc, mass_term, face_term):
    extent = viscosity.shape
    summed = mass_term * values
    for offset in neighbours:
        beside = window(padded_visc, offset, extent)
        across = window(padded_values, offset, extent)
        summed = summed + face_term * (viscosity + beside) * (values - across)
    return summed


def diagonal_of(viscosity, padded_visc, mass_term, face_term):
    summed = jnp.full(viscosity.shape, mass_term, jnp.float32)
    for offset in neighbours:
        summed = summed + face_term * (viscosity + window(padded_visc, offset, viscosity.shape))
    return summed


def restrict(values):
    extent = values.shape
    return values.reshape(extent[0], extent[1] // 2, 2, extent[2] // 2, 2, extent[3] // 2, 2).sum(
        axis=(2, 4, 6)
    )


def prolong(values):
    return jnp.repeat(jnp.repeat(jnp.repeat(values, 2, axis=1), 2, axis=2), 2, axis=3)


def coarsen(viscosity):
    extent = viscosity.shape
    return viscosity.reshape(extent[0] // 2, 2, extent[1] // 2, 2, extent[2] // 2, 2).mean(
        axis=(1, 3, 5)
    )


def sweeps(coarse_rhs, diagonal, applier):
    correction = relaxation * coarse_rhs / diagonal
    for counter in range(CSWEEPS - 1):
        correction = correction + relaxation * (coarse_rhs - applier(correction)) / diagonal
    return correction


def precond_product(residual, precond):
    return lax.psum(jnp.sum(residual * precond), ("gx", "gy", "gz"))


def shards(forcing, viscosity):
    padded_visc = with_halo(viscosity, (("gx", 0), ("gy", 1), ("gz", 2)), 1)
    fine_diag = diagonal_of(viscosity, padded_visc, reaction, 0.5)
    coarse_visc = coarsen(viscosity)

    def fine_apply(values):
        padded = with_halo(values, (("gx", 1), ("gy", 2), ("gz", 3)), 1)
        return viscous(values, padded, viscosity, padded_visc, reaction, 0.5)

    group_visc = lax.all_gather(coarse_visc, "gz", axis=2, tiled=True)
    group_pad = with_halo(group_visc, (("gx", 0), ("gy", 1)), 1)
    group_pad = jnp.pad(group_pad, ((0, 0), (0, 0), (1, 1)))
    group_diag = diagonal_of(group_visc, group_pad, 8.0 * reaction, 2.0)
    depth_local = coarse_visc.shape[2]
    offset_z = lax.axis_index("gz") * depth_local

    def group_apply(values):
        padded = with_halo(values, (("gx", 1), ("gy", 2)), 1)
        padded = jnp.pad(padded, ((0, 0), (0, 0), (0, 0), (1, 1)))
        return viscous(values, padded, group_visc, group_pad, 8.0 * reaction, 2.0)

    def coarse_solve(coarse_rhs):
        whole_line = lax.all_gather(coarse_rhs, "gz", axis=3, tiled=True)
        correction = sweeps(whole_line, group_diag, group_apply)
        return lax.dynamic_slice_in_dim(correction, offset_z, depth_local, 3)

    def precondition(residual):
        smoothed = relaxation * residual / fine_diag
        defect = residual - fine_apply(smoothed)
        correction = coarse_solve(restrict(defect))
        smoothed = smoothed + prolong(correction)
        return smoothed + relaxation * (residual - fine_apply(smoothed)) / fine_diag

    solution = jnp.zeros_like(forcing)
    residual = forcing
    precond = precondition(residual)
    product = precond_product(residual, precond)
    direction = precond
    for iteration in range(ITERS):
        applied = fine_apply(direction)
        alpha_step = product / lax.psum(jnp.sum(direction * applied), ("gx", "gy", "gz"))
        solution = solution + alpha_step * direction
        residual = residual - alpha_step * applied
        if iteration + 1 < ITERS:
            precond = precondition(residual)
            product_next = precond_product(residual, precond)
            direction = precond + product_next / product * direction
            product = product_next
    return (solution, residual)


def solution(mesh):
    return jax.shard_map(
        shards,
        mesh=mesh,
        in_specs=(P(None, "gx", "gy", "gz"), P("gx", "gy", "gz")),
        out_specs=(P(None, "gx", "gy", "gz"), P(None, "gx", "gy", "gz")),
        check_vma=False,
    )
```

profile of v0, /device:TPU:0, one launch (start us, length us, event | category | flops | bytes accessed | tf_op | source)
XLA Modules:
  0.0 754.0 jit_solution(5678509347087031177)
XLA Ops:
  1.3 4.9 collective-permute-start.1
  7.5 6.3 reshape.58
  21.4 7.2 all_gather.13
  32.5 4.5 collective-permute-start.13
  38.6 4.5 collective-permute-start.7
  44.5 4.5 collective-permute-start.15
  50.4 4.5 collective-permute-start.9
  66.7 13.9 %reshape.57 = f32[3,4,2,8,2,64,2]{6,5,4,3,2,1,0:T(8,128)} reshape(f32[3,8,16,128]{3,2,1,0:T(8,128)S(1)} %fusion.162) | data formatting | bytes 393216 | tf_op jit(solution)/shard_map/reshape | solution.py:56
  80.7 5.5 reduce_sum.90
  86.4 19.3 %all_gather.12 = f32[3,4,8,256]{2,1,0,3:T(4,128)S(1)} all-gather(f32[3,4,8,64]{2,1,0,3:T(4,128)S(1)} %copy.996), channel_id=1, replica_groups=mesh['gx'=2,'gy'=4,'gz'=4] {'gz'}, dimensions={3}, use_global_device_ids=true | all-gather | bytes 122880 | tf_op jit(solution)/shard_map/all_gather | solution.py:105
  106.3 4.5 collective-permute-start.17
  204.8 46.7 %all-reduce.10 = (f32[]{:T(128)}, f32[]{:T(128)}) all-reduce(f32[]{:T(128)} %get-tuple-element.13, f32[]{:T(128)} %get-tuple-element.12), channel_id=1, replica_groups=mesh['gx'=2,'gy'=4,'gz'=4] {'gx','gy','gz'}, use_global_device_ids=true, to_apply=%region_3.4 | all-reduce | flops 2 | bytes 16 | tf_op jit(solution)/shard_map/psum | solution.py:80
  278.6 13.9 %reshape.62 = f32[3,4,2,8,2,64,2]{6,5,4,3,2,1,0:T(8,128)} reshape(f32[3,8,16,128]{3,2,1,0:T(8,128)S(1)} %fusion.103) | data formatting | bytes 393216 | tf_op jit(solution)/shard_map/reshape | solution.py:56
  292.6 5.5 reduce_sum.94
  298.3 18.5 %all_gather.14 = f32[3,4,8,256]{2,1,0,3:T(4,128)S(1)} all-gather(f32[3,4,8,64]{2,1,0,3:T(4,128)S(1)} %copy.1016), channel_id=1, replica_groups=mesh['gx'=2,'gy'=4,'gz'=4] {'gz'}, dimensions={3}, use_global_device_ids=true | all-gather | bytes 122880 | tf_op jit(solution)/shard_map/all_gather | solution.py:105
  389.3 41.5 %psum.44 = f32[]{:T(128)} all-reduce(f32[]{:T(128)} %get-tuple-element.24), channel_id=1, replica_groups=mesh['gx'=2,'gy'=4,'gz'=4] {'gx','gy','gz'}, use_global_device_ids=true, to_apply=%region_8.9 | all-reduce | flops 1 | bytes 8 | tf_op jit(solution)/shard_map/psum | solution.py:80
  432.1 4.4 collective-permute-start.65
  458.5 43.7 %psum.45 = f32[]{:T(128)} all-reduce(f32[]{:T(128)} %get-tuple-element.22), channel_id=1, replica_groups=mesh['gx'=2,'gy'=4,'gz'=4] {'gx','gy','gz'}, use_global_device_ids=true, to_apply=%region_10.11 | all-reduce | flops 1 | bytes 8 | tf_op jit(solution)/shard_map/psum | solution.py:123
  503.6 4.4 collective-permute-start.71
  528.8 13.9 %reshape.66 = f32[3,4,2,8,2,64,2]{6,5,4,3,2,1,0:T(8,128)} reshape(f32[3,8,16,128]{3,2,1,0:T(8,128)S(1)} %fusion.44) | data formatting | bytes 393216 | tf_op jit(solution)/shard_map/reshape | solution.py:56
  542.8 5.5 reduce_sum.97
  548.5 18.5 %all_gather.15 = f32[3,4,8,256]{2,1,0,3:T(4,128)S(1)} all-gather(f32[3,4,8,64]{2,1,0,3:T(4,128)S(1)} %copy.1024), channel_id=1, replica_groups=mesh['gx'=2,'gy'=4,'gz'=4] {'gz'}, dimensions={3}, use_global_device_ids=true | all-gather | bytes 122880 | tf_op jit(solution)/shard_map/all_gather | solution.py:105
  638.3 41.5 %psum.46 = f32[]{:T(128)} all-reduce(f32[]{:T(128)} %get-tuple-element.18), channel_id=1, replica_groups=mesh['gx'=2,'gy'=4,'gz'=4] {'gx','gy','gz'}, use_global_device_ids=true, to_apply=%region_13.14 | all-reduce | flops 1 | bytes 8 | tf_op jit(solution)/shard_map/psum | solution.py:80
  707.5 43.7 %psum.47 = f32[]{:T(128)} all-reduce(f32[]{:T(128)} %get-tuple-element.16), channel_id=1, replica_groups=mesh['gx'=2,'gy'=4,'gz'=4] {'gx','gy','gz'}, use_global_device_ids=true, to_apply=%region_15.16 | all-reduce | flops 1 | bytes 8 | tf_op jit(solution)/shard_map/psum | solution.py:123
  (341 shorter events, 363.4 us)
Async XLA Ops:
  1.3 15.2 %collective-permute-start.1 = (f32[1,16,128]{2,1,0:T(8,128)S(1)}, f32[1,16,128]{2,1,0:T(8,128)S(1)}, u32[]{:S(2)}, u32[]{:S(2)}) collective-permute-start(f32[1,16,128]{2,1,0:T(8,128)S(1)} %get-tuple-element.143), channel_id=1, source_target_pairs={{0,16},{1,17},{2,18},{3,19},{4,20},{5,21},{6,22},{7,23},{8,24},{9,... | collective-permute-start | bytes 24584 | tf_op jit(solution)/shard_map/ppermute | solution.py:22
  6.2 10.4 %collective-permute-start = (f32[1,16,128]{2,1,0:T(8,128)S(1)}, f32[1,16,128]{2,1,0:T(8,128)S(1)}, u32[]{:S(2)}, u32[]{:S(2)}) collective-permute-start(f32[1,16,128]{2,1,0:T(8,128)S(1)} %get-tuple-element.144), channel_id=1, source_target_pairs={{16,0},{17,1},{18,2},{19,3},{20,4},{21,5},{22,6},{23,7},{24,8},{25... | collective-permute-start | bytes 24584 | tf_op jit(solution)/shard_map/ppermute | solution.py:23
  16.6 12.1 %collective-permute-start.3 = (f32[10,1,128]{2,1,0:T(1,128)S(1)}, f32[10,1,128]{2,1,0:T(1,128)S(1)}, u32[]{:S(2)}, u32[]{:S(2)}) collective-permute-start(f32[10,1,128]{2,1,0:T(1,128)S(1)} %get-tuple-element.141), channel_id=1, source_target_pairs={{0,4},{4,8},{8,12},{1,5},{5,9},{9,13},{2,6},{6,10},{10,14},{3,7},{... | collective-permute-start | bytes 15368 | tf_op jit(solution)/shard_map/ppermute | solution.py:22
  20.1 8.7 %collective-permute-start.2 = (f32[10,1,128]{2,1,0:T(1,128)S(1)}, f32[10,1,128]{2,1,0:T(1,128)S(1)}, u32[]{:S(2)}, u32[]{:S(2)}) collective-permute-start(f32[10,1,128]{2,1,0:T(1,128)S(1)} %get-tuple-element.142), channel_id=1, source_target_pairs={{4,0},{8,4},{12,8},{5,1},{9,5},{13,9},{6,2},{10,6},{14,10},{7,3},{... | collective-permute-start | bytes 15368 | tf_op jit(solution)/shard_map/ppermute | solution.py:23
  28.9 9.4 %collective-permute-start.5 = (f32[10,18,1]{2,1,0:T(8,128)S(1)}, f32[10,18,1]{2,1,0:T(8,128)S(1)}, u32[]{:S(2)}, u32[]{:S(2)}) collective-permute-start(f32[10,18,1]{2,1,0:T(8,128)S(1)} %get-tuple-element.121), channel_id=1, source_target_pairs={{0,1},{1,2},{2,3},{4,5},{5,6},{6,7},{8,9},{9,10},{10,11},{12,13},{... | collective-permute-start | bytes 2168 | tf_op jit(solution)/shard_map/ppermute | solution.py:22
  31.2 7.2 collective-permute-start.4
  32.5 11.9 %collective-permute-start.13 = (f32[1,8,256]{2,1,0:T(8,128)S(1)}, f32[1,8,256]{2,1,0:T(8,128)S(1)}, u32[]{:S(2)}, u32[]{:S(2)}) collective-permute-start(f32[1,8,256]{2,1,0:T(8,128)S(1)} %get-tuple-element.147), channel_id=1, source_target_pairs={{0,16},{1,17},{2,18},{3,19},{4,20},{5,21},{6,22},{7,23},{8,24},{9,... | collective-permute-start | bytes 24584 | tf_op jit(solution)/shard_map/ppermute | solution.py:22
  37.0 7.4 collective-permute-start.12
  38.6 11.7 %collective-permute-start.7 = (f32[3,1,16,128]{3,2,1,0:T(8,128)S(1)}, f32[3,1,16,128]{3,2,1,0:T(8,128)S(1)}, u32[]{:S(2)}, u32[]{:S(2)}) collective-permute-start(f32[3,1,16,128]{3,2,1,0:T(8,128)S(1)} %get-tuple-element.101), channel_id=1, source_target_pairs={{0,16},{1,17},{2,18},{3,19},{4,20},{5,21},{6,22},{7,23},{8,24},{9,... | collective-permute-start | bytes 73736 | tf_op jit(solution)/shard_map/ppermute | solution.py:22
  43.1 7.2 collective-permute-start.6
  44.5 11.8 %collective-permute-start.15 = (f32[6,1,256]{2,1,0:T(1,128)S(1)}, f32[6,1,256]{2,1,0:T(1,128)S(1)}, u32[]{:S(2)}, u32[]{:S(2)}) collective-permute-start(f32[6,1,256]{2,1,0:T(1,128)S(1)} %get-tuple-element.145), channel_id=1, source_target_pairs={{0,4},{4,8},{8,12},{1,5},{5,9},{9,13},{2,6},{6,10},{10,14},{3,7},{... | collective-permute-start | bytes 18440 | tf_op jit(solution)/shard_map/ppermute | solution.py:22
  49.0 7.2 collective-permute-start.14
  50.4 6.0 collective-permute-start.9
  106.3 6.1 collective-permute-start.17
  144.9 5.7 collective-permute-start.24
  163.5 5.7 collective-permute-start.28
  252.9 5.9 collective-permute-start.41
  257.2 5.7 collective-permute-start.40
  335.1 5.7 collective-permute-start.50
  432.1 5.9 collective-permute-start.65
  503.6 5.9 collective-permute-start.71
  508.0 5.7 collective-permute-start.70
  601.4 5.7 collective-permute-start.84
  681.1 5.9 collective-permute-start.95
  (80 other events, 421.1 us)
where the time goes:
time: 757 us; the launch traced here: 754 us
  blocking collectives  281 us (37%)
  starting transfers between devices  208 us (27%)
  waiting for transfers between devices  164 us (22%)
  local copies, waits for them, and re-layouts  60.2 us (8%)
  other arithmetic  32.7 us (4%)
  between operations  8.96 us (1%)
    ppermute x50, waiting for transfers between devices, with_halo(): after = lax.ppermute(initial, axis, down)  147 us
    ppermute x50, starting transfers between devices, with_halo(): before = lax.ppermute(last, axis, up)  143 us
    psum x3, blocking collectives, precond_product(): return lax.psum(jnp.sum(residual * precond), ('gx', 'gy', 'gz'))  130 us
    psum x2, blocking collectives, shards(): lax.psum(jnp.sum(direction * applied), ('gx', 'gy', 'gz'))  87.4 us
    ppermute x50, starting transfers between devices, with_halo(): after = lax.ppermute(initial, axis, down)  64.8 us
    all_gather x3, blocking collectives, coarse_solve(): whole_line = lax.all_gather(coarse_rhs, 'gz', axis=3, tiled=True)  56.3 us
    reshape x3, local copies, waits for them, and re-layouts, restrict(): values.reshape(extent[0], extent[1] // 2, 2, extent[2] // 2, 2, extent[3]...  41.8 us
    ppermute x50, waiting for transfers between devices, with_halo(): before = lax.ppermute(last, axis, up)  16.6 us
  transfers between devices with their start and end apart: 100, of which 77 were waited for; matrix products, arithmetic and copies ran while one was open for 1% of the time, Pallas kernels for 0%

commit v1 on v0

v1 whole, which is shorter than its diff:
```python
import functools
import jax
import jax.numpy as jnp
from jax import lax
from jax.experimental import pallas as pl
from jax.experimental.pallas import tpu as pltpu
from jax.sharding import PartitionSpec as P

ITERS = 3
CSWEEPS = 4
REACTION = 1.0
RELAX = 2.0 / 3.0

STEP = 2 * (CSWEEPS - 1) + 4
HALO = ITERS * STEP
CHUNK = 16


def lane_iota(shape):
    return lax.broadcasted_iota(jnp.int32, shape, len(shape) - 1)


def sub_iota(shape):
    return lax.broadcasted_iota(jnp.int32, shape, len(shape) - 2)


def roll(v, shift, dim):
    size = v.shape[dim]
    return pltpu.roll(v, shift % size, dim)


def swap_blocks(v, count, width):
    sub, lane = sub_iota(v.shape), lane_iota(v.shape)
    step = 1
    while step < count:
        low = (sub // step) % 2 == 1
        high = (lane // (step * width)) % 2 == 1
        rows, lanes = v.ndim - 2, v.ndim - 1
        from_left = roll(roll(v, step, rows), -step * width, lanes)
        from_right = roll(roll(v, -step, rows), step * width, lanes)
        v = jnp.where(low == high, v, jnp.where(low, from_left, from_right))
        step *= 2
    return v


def chunked(lo, hi, n, body):
    n = min(n, hi - lo)
    count = -(-(hi - lo) // n)
    if count == 1:
        body(lo, n)
        return

    @pl.loop(0, count)
    def _(i):
        body(jnp.minimum(lo + i * n, hi - n), n)


class Sizes:
    def __init__(self, mesh, comps, xl, yl, zl):
        self.gx, self.gy, self.gz = (mesh[a] for a in ("gx", "gy", "gz"))
        self.comps, self.xl, self.yl, self.zl = comps, xl, yl, zl
        self.group = self.gx * self.gy
        self.planes = zl // self.gx
        self.rows = self.gx * xl // 2
        self.width = self.gy * yl
        self.lanes = xl * yl
        self.window = self.planes + 2 * HALO
        self.hops = []
        left = HALO
        while left > 0:
            self.hops.append(min(left, self.planes))
            left -= self.planes
        assert comps <= self.gy and xl == 2 * self.gy
        assert zl % (2 * self.gx) == 0 and 2 * self.width == self.lanes


def slab_of(sz, i):
    z, k = divmod(i, sz.gx)
    return (k if z % 2 == 0 else sz.gx - 1 - k) * sz.gz + z


def to_slab(sz, x, shift):
    n = sz.gx * sz.gz
    perm = [(slab_of(sz, i), slab_of(sz, i + shift)) for i in range(n) if 0 <= i + shift < n]
    return lax.ppermute(x, ("gx", "gz"), perm)


def x_order(sz):
    return list(range(0, sz.xl, 2)) + list(range(1, sz.xl, 2))


def part_of(sz, half):
    odd = lax.axis_index("gz") % 2
    return jnp.where(odd == 1, sz.gx - 1 - half, half)


def pack_kernel(sz, f_ref, v_ref, out_ref):
    def turned(at):
        return jnp.concatenate([at(x) for x in x_order(sz)], axis=0).T

    visc = turned(lambda x: v_ref[x])
    zero = jnp.zeros((sz.planes, sz.lanes), jnp.float32)
    for c in range(sz.gy):
        field = turned(lambda x: f_ref[c, x]) if c < sz.comps else None
        for half in range(sz.gx):
            dest = part_of(sz, half) * sz.gy + c
            cut = slice(half * sz.planes, (half + 1) * sz.planes)
            out_ref[dest, 0] = zero if field is None else field[cut]
            out_ref[dest, 1] = zero if field is None else visc[cut]


def planes_kernel(sz, in_ref, main_ref, *rest):
    edges, scr = rest[:-1], rest[-1]
    for a in range(2):
        for src in range(sz.group):
            scr[pl.ds(src, sz.planes, stride=sz.group), :] = in_ref[src, a]

        def body(p, n):
            rows = pl.multiple_of(p * sz.group, 8)
            v = scr[pl.ds(rows, n * sz.group), :].reshape(n, sz.group, sz.lanes)
            main_ref[a, pl.ds(p, n)] = swap_blocks(v, sz.gy, sz.yl)

        chunked(0, sz.planes, CHUNK, body)
        k = 0
        for count in sz.hops:
            if count < sz.planes:
                edges[k][a] = main_ref[a, 0:count]
                edges[k + 1][a] = main_ref[a, sz.planes - count : sz.planes]
                k += 2


def basis_kernel(sz, *refs):
    nh = len(sz.hops)
    main_ref, halos = refs[0], refs[1 : 1 + 2 * nh]
    u_out, rho_out, gram_out = refs[1 + 2 * nh : 4 + 2 * nh]
    it = iter(refs[4 + 2 * nh :])
    visc, cin, cout, cyp, cym, mass, cz, od = (next(it) for _ in range(8))
    cv, ccx, ccyp, ccym, cmass, ccz, cod, rhs, c0, c1 = (next(it) for _ in range(10))
    sm, sm2 = next(it), next(it)
    rhos = [next(it) for _ in range(ITERS + 1)]
    us = [next(it) for _ in range(ITERS)]

    H, N, W = HALO, sz.planes, sz.window
    for a, ref in ((0, rhos[0]), (1, visc)):
        ref[H : H + N] = main_ref[a]
        at_lo, at_hi = H, H + N
        for j, count in enumerate(sz.hops):
            ref[at_lo - count : at_lo] = halos[2 * j][a]
            ref[at_hi : at_hi + count] = halos[2 * j + 1][a]
            at_lo, at_hi = at_lo - count, at_hi + count

    plane = (1, sz.rows, sz.lanes)
    lane, sub = lane_iota(plane), sub_iota(plane)
    upper = lane >= sz.width
    y = lane % sz.width
    half_y = sz.width // 2

    def x_other(swapped):
        return jnp.where(upper, roll(swapped, -1, 1), roll(swapped, 1, 1))

    edge_out = (upper & (sub == sz.rows - 1)) | (~upper & (sub == 0))
    edge_yp, edge_ym = y == sz.width - 1, y == 0

    def split(total, edge):
        return jnp.where(edge, 0.0, total)

    def faces_z(ref, p, n, term):
        a, b = ref[pl.ds(p, n)], ref[pl.ds(p + 1, n)]
        return jnp.where((a > 0) & (b > 0), term * (a + b), 0.0)

    def fine_faces(p, n):
        cz[pl.ds(p, n)] = faces_z(visc, p, n, 0.5)

    chunked(0, W - 1, CHUNK, fine_faces)

    def fine_coeffs(p, n):
        v = visc[pl.ds(p, n)]
        before, after = visc[pl.ds(p - 1, n)], visc[pl.ds(p + 1, n)]
        swapped = roll(v, sz.width, 2)
        half = 0.5 * v
        inner = half + 0.5 * swapped
        outer = jnp.where(edge_out, 0.0, half + 0.5 * x_other(swapped))
        yp = jnp.where(edge_yp, 0.0, half + 0.5 * roll(v, -1, 2))
        ym = jnp.where(edge_ym, 0.0, half + 0.5 * roll(v, 1, 2))
        m = REACTION + jnp.where(edge_out, half, 0.0) + jnp.where(edge_yp | edge_ym, half, 0.0)
        m = m + jnp.where(before > 0, 0.0, half) + jnp.where(after > 0, 0.0, half)
        cin[pl.ds(p, n)] = inner
        cout[pl.ds(p, n)] = outer
        cyp[pl.ds(p, n)] = yp
        cym[pl.ds(p, n)] = ym
        mass[pl.ds(p, n)] = m
        od[pl.ds(p, n)] = RELAX / (m + inner + outer + yp + ym + cz[pl.ds(p - 1, n)] + cz[pl.ds(p, n)])

    chunked(1, W - 1, CHUNK, fine_coeffs)

    def gather_block(fine, n):
        t = fine.reshape(n, 2, sz.rows, sz.lanes)
        t = t[:, 0] + t[:, 1]
        t = t + roll(t, sz.width, 2)
        return t + jnp.where(lane % 2 == 0, roll(t, -1, 2), roll(t, 1, 2))

    def coarse_visc(p, n):
        cv[pl.ds(p, n)] = 0.125 * gather_block(visc[pl.ds(2 * p, 2 * n)], n)

    chunked(0, W // 2, CHUNK // 2, coarse_visc)

    def coarse_faces(p, n):
        ccz[pl.ds(p, n)] = faces_z(cv, p, n, 2.0)

    chunked(0, W // 2 - 1, CHUNK, coarse_faces)
    cedge_yp, cedge_ym = y >= sz.width - 2, y < 2

    def coarse_coeffs(p, n):
        v = cv[pl.ds(p, n)]
        before, after = cv[pl.ds(p - 1, n)], cv[pl.ds(p + 1, n)]
        twice = 2.0 * v
        xp = jnp.where(sub == sz.rows - 1, 0.0, twice + 2.0 * roll(v, -1, 1))
        yp = jnp.where(cedge_yp, 0.0, twice + 2.0 * roll(v, -2, 2))
        ym = jnp.where(cedge_ym, 0.0, twice + 2.0 * roll(v, 2, 2))
        m = 8.0 * REACTION + jnp.where(sub == 0, twice, 0.0) + jnp.where(sub == sz.rows - 1, twice, 0.0)
        m = m + jnp.where(cedge_yp, twice, 0.0) + jnp.where(cedge_ym, twice, 0.0)
        m = m + jnp.where(before > 0, 0.0, twice) + jnp.where(after > 0, 0.0, twice)
        ccx[pl.ds(p, n)] = xp
        ccyp[pl.ds(p, n)] = yp
        ccym[pl.ds(p, n)] = ym
        cmass[pl.ds(p, n)] = m
        cod[pl.ds(p, n)] = RELAX / (m + xp + roll(xp, 1, 1) + yp + ym + ccz[pl.ds(p - 1, n)] + ccz[pl.ds(p, n)])

    chunked(1, W // 2 - 1, CHUNK, coarse_coeffs)

    def fine_apply(ref, p, n):
        ext = ref[pl.ds(p - 1, n + 2)]
        v = ext[1 : n + 1]
        flux = cz[pl.ds(p - 1, n + 1)] * (ext[: n + 1] - ext[1:])
        swapped = roll(v, sz.width, 2)
        out = mass[pl.ds(p, n)] * v + (flux[1:] - flux[:n])
        out = out + cyp[pl.ds(p, n)] * (v - roll(v, -1, 2)) + cym[pl.ds(p, n)] * (v - roll(v, 1, 2))
        return out + cin[pl.ds(p, n)] * (v - swapped) + cout[pl.ds(p, n)] * (v - x_other(swapped))

    def coarse_apply(ref, p, n):
        ext = ref[pl.ds(p - 1, n + 2)]
        v = ext[1 : n + 1]
        flux = ccz[pl.ds(p - 1, n + 1)] * (ext[: n + 1] - ext[1:])
        fx = ccx[pl.ds(p, n)] * (v - roll(v, -1, 1))
        out = cmass[pl.ds(p, n)] * v + (flux[1:] - flux[:n]) + (fx - roll(fx, 1, 1))
        return out + ccyp[pl.ds(p, n)] * (v - roll(v, -2, 2)) + ccym[pl.ds(p, n)] * (v - roll(v, 2, 2))

    def spread(reach, n, body, unit=1):
        chunked((H - reach) // unit, (H + N + reach) // unit, n, body)

    for k in range(ITERS):
        reach = HALO - 1 - k * STEP
        rho, rho_next, u = rhos[k], rhos[k + 1], us[k]

        def smooth(p, n):
            sm[pl.ds(p, n)] = od[pl.ds(p, n)] * rho[pl.ds(p, n)]

        spread(reach, CHUNK, smooth)

        def restricted(p, n):
            defect = rho[pl.ds(2 * p, 2 * n)] - fine_apply(sm, 2 * p, 2 * n)
            b = gather_block(defect, n)
            rhs[pl.ds(p, n)] = b
            c0[pl.ds(p, n)] = cod[pl.ds(p, n)] * b

        spread(reach - 1, CHUNK // 2, restricted, 2)
        old, new = c0, c1
        for sweep in range(1, CSWEEPS):

            def relax(p, n):
                at = pl.ds(p, n)
                new[at] = old[at] + cod[at] * (rhs[at] - coarse_apply(old, p, n))

            spread(reach - 1 - 2 * sweep, CHUNK, relax, 2)
            old, new = new, old
        reach = reach - 1 - 2 * (CSWEEPS - 1)

        def prolonged(p, n):
            c = old[pl.ds(p, n)]
            fine = jnp.stack([c, c], axis=1).reshape(2 * n, sz.rows, sz.lanes)
            sm2[pl.ds(2 * p, 2 * n)] = sm[pl.ds(2 * p, 2 * n)] + fine

        spread(reach, CHUNK // 2, prolonged, 2)

        def smoothed(p, n):
            at = pl.ds(p, n)
            u[at] = sm2[at] + od[at] * (rho[at] - fine_apply(sm2, p, n))

        spread(reach - 1, CHUNK, smoothed)

        def descend(p, n):
            rho_next[pl.ds(p, n)] = rho[pl.ds(p, n)] - fine_apply(u, p, n)

        spread(reach - 2, CHUNK, descend)

    pairs = [(j, k) for j in range(ITERS + 1) for k in range(ITERS)]

    def products(i, sums):
        p = H + i
        rv = [r[p] for r in rhos]
        uv = [u[p] for u in us]
        for k in range(ITERS):
            u_out[k, i] = uv[k]
            rho_out[k, i] = rv[k + 1]
        return tuple(s + rv[j] * uv[k] for s, (j, k) in zip(sums, pairs))

    zero = jnp.zeros((sz.rows, sz.lanes), jnp.float32)
    sums = lax.fori_loop(0, N, products, (zero,) * len(pairs), unroll=4)
    wide = -(-len(pairs) // 8) * 8
    rows = [jnp.sum(s, axis=0, keepdims=True) for s in sums]
    rows = jnp.concatenate(rows + [jnp.zeros((wide - len(rows), sz.lanes), jnp.float32)], axis=0)
    total = jnp.broadcast_to(jnp.sum(rows, axis=1, keepdims=True), rows.shape)
    line = jnp.sum(jnp.where(sub_iota(rows.shape) == lane_iota(rows.shape), total, 0.0), axis=0, keepdims=True)
    gram_out[...] = jnp.broadcast_to(line[None], gram_out.shape)


def combine_kernel(sz, gram_ref, main_ref, u_ref, rho_ref, out_ref, scr):
    line = jnp.sum(gram_ref[...], axis=0)
    lane = lane_iota(line.shape)

    def entry(j, k):
        picked = jnp.where(lane == j * ITERS + k, line, 0.0)
        return jnp.broadcast_to(jnp.sum(picked, axis=1, keepdims=True), line.shape)

    g = [[entry(j, k) for k in range(ITERS)] for j in range(ITERS + 1)]
    zero = jnp.zeros_like(line)
    one = jnp.ones_like(line)

    def form(left, right, matrix):
        total = zero
        for j, a in enumerate(left):
            for k, b in enumerate(right):
                total = total + a * b * matrix(j, k)
        return total

    res = [one]
    direction = [one]
    sol = [zero] * ITERS
    product = g[0][0]
    for i in range(ITERS):
        alpha = product / form(direction, direction, lambda j, k: g[k][j] - g[k + 1][j])
        for k, b in enumerate(direction):
            sol[k] = sol[k] + alpha * b
        res = res + [zero]
        for k, b in enumerate(direction):
            res[k] = res[k] - alpha * b
            res[k + 1] = res[k + 1] + alpha * b
        if i + 1 < ITERS:
            following = form(res, res, lambda j, k: g[j][k])
            beta = following / product
            direction = [a + beta * b for a, b in zip(res, direction + [zero])]
            product = following

    sol = [s.reshape(1, 1, sz.lanes) for s in sol]
    res = [s.reshape(1, 1, sz.lanes) for s in res]

    for a in range(2):

        def body(p, n):
            at = pl.ds(p, n)
            if a == 0:
                v = sum(sol[k] * u_ref[k, at] for k in range(ITERS))
            else:
                v = res[0] * main_ref[0, at] + sum(res[k + 1] * rho_ref[k, at] for k in range(ITERS))
            v = swap_blocks(v, sz.gy, sz.yl)
            rows = pl.multiple_of(p * sz.group, 8)
            scr[pl.ds(rows, n * sz.group), :] = v.reshape(n * sz.group, sz.lanes)

        chunked(0, sz.planes, CHUNK, body)
        for dest in range(sz.group):
            out_ref[dest, a] = scr[pl.ds(dest, sz.planes, stride=sz.group), :]


def unpack_kernel(sz, in_ref, sol_ref, res_ref):
    for a, out in ((0, sol_ref), (1, res_ref)):
        for c in range(sz.comps):
            halves = [in_ref[part_of(sz, half) * sz.gy + c, a] for half in range(sz.gx)]
            turned = jnp.concatenate(halves, axis=0).T
            for i, x in enumerate(x_order(sz)):
                out[c, x] = turned[i * sz.yl : (i + 1) * sz.yl]


def vmem(count):
    return [pl.BlockSpec(memory_space=pltpu.VMEM)] * count


def call(kernel, sz, ins, outs, scratch=(), name=None):
    outs = [jax.ShapeDtypeStruct(s, jnp.float32) for s in outs]
    return pl.pallas_call(
        functools.partial(kernel, sz),
        in_specs=vmem(len(ins)),
        out_specs=vmem(len(outs)),
        out_shape=outs,
        scratch_shapes=[pltpu.VMEM(s, jnp.float32) for s in scratch],
        compiler_params=pltpu.CompilerParams(vmem_limit_bytes=56 * 2**20),
        name=name,
    )(*ins)


def shards(mesh, forcing, viscosity):
    comps, xl, yl, zl = forcing.shape
    sz = Sizes(mesh, comps, xl, yl, zl)
    N, W = sz.planes, sz.window
    plane = (sz.rows, sz.lanes)
    group_shape = (sz.group, 2, N, sz.lanes)
    (packed,) = call(pack_kernel, sz, [forcing, viscosity], [group_shape], name="pack")
    packed = lax.all_to_all(packed, ("gx", "gy"), 0, 0)
    edge_shapes = [(2, c) + plane for c in sz.hops if c < N for _ in range(2)]
    main, *edges = call(
        planes_kernel, sz, [packed], [(2, N) + plane] + edge_shapes, [(N * sz.group, sz.lanes)], name="planes"
    )
    halos = []
    for j, count in enumerate(sz.hops):
        first, last = (edges.pop(0), edges.pop(0)) if count < N else (main, main)
        halos += [to_slab(sz, last, j + 1), to_slab(sz, first, -(j + 1))]
    devices = sz.group * sz.gz
    fine, coarse = (W,) + plane, (W // 2,) + plane
    u, rho, gram = call(
        basis_kernel,
        sz,
        [main] + halos,
        [(ITERS, N) + plane, (ITERS, N) + plane, (devices, 1, sz.lanes)],
        [fine] * 8 + [coarse] * 10 + [fine] * (2 + 2 * ITERS + 1),
        name="basis",
    )
    gram = lax.all_to_all(gram, ("gx", "gy", "gz"), 0, 0)
    (mixed,) = call(
        combine_kernel, sz, [gram, main, u, rho], [group_shape], [(N * sz.group, sz.lanes)], name="combine"
    )
    mixed = lax.all_to_all(mixed, ("gx", "gy"), 0, 0)
    return tuple(call(unpack_kernel, sz, [mixed], [forcing.shape, forcing.shape], name="unpack"))


def solution(mesh):
    spec = P(None, "gx", "gy", "gz")
    return jax.shard_map(
        functools.partial(shards, dict(mesh.shape)),
        mesh=mesh,
        in_specs=(spec, P("gx", "gy", "gz")),
        out_specs=(spec, spec),
        check_vma=False,
    )
```

time: 757 us -> 96.7 us (0.13)
  blocking collectives: 281 us -> 52.8 us
  starting transfers between devices: 208 us -> 3.76 us
  waiting for transfers between devices: 164 us -> 7 us
  local copies, waits for them, and re-layouts: 60.2 us -> 0.68 us
  other arithmetic: 32.7 us -> 0 us
  Pallas kernels: 0 us -> 31.3 us
  between operations: 8.96 us -> 0.65 us
    psum x5 -> x0, blocking collectives: 217 us -> none  [the longest x3 130 us: precond_product(): return lax.psum(jnp.sum(residual * precond), ('gx', 'gy', 'gz'))]
    ppermute x100 -> x2, starting transfers between devices: 208 us -> 3.76 us  [to_slab(): return lax.ppermute(x, ('gx', 'gz'), perm)]
    ppermute x100 -> x2, waiting for transfers between devices: 164 us -> 7 us  [to_slab(): return lax.ppermute(x, ('gx', 'gz'), perm)]
    all_gather x4 -> x0, blocking collectives: 63.5 us -> none  [the longest x3 56.3 us: coarse_solve(): whole_line = lax.all_gather(coarse_rhs, 'gz', axis=3, tiled=True)]
    all_to_all x0 -> x3, blocking collectives: none -> 52.8 us  [the longest x1 22.8 us: shards(): packed = lax.all_to_all(packed, ('gx', 'gy'), 0, 0)]
    reshape x10 -> x0, local copies, waits for them, and re-layouts: 52.2 us -> none  [the longest x3 41.8 us: restrict(): values.reshape(extent[0], extent[1] // 2, 2, extent[2] // 2, 2, extent[3]...]
    pallas_call x0 -> x5, Pallas kernels: none -> 31.3 us  [call(): pl.pallas_call(functools.partial(kernel, sz), in_specs=vmem(len(ins)), ou...]
    reduce_sum x9 -> x0, other arithmetic: 23.7 us -> none  [the longest x3 16.5 us: restrict(): values.reshape(extent[0], extent[1] // 2, 2, extent[2] // 2, 2, extent[3]...]
  transfers between devices with their start and end apart: 100 -> 2, of which waited for: 77 -> 2; matrix products, arithmetic and copies ran while one was open for 1% -> 0% of each run, Pallas kernels for 0% -> 0%
where the time goes in v1:
time: 96.7 us; the launch traced here: 96.2 us
  blocking collectives  52.8 us (55%)
  Pallas kernels  31.3 us (32%)
  waiting for transfers between devices  7 us (7%)
  starting transfers between devices  3.76 us (4%)
    pallas_call x5, Pallas kernels, call(): pl.pallas_call(functools.partial(kernel, sz), in_specs=vmem(len(ins)), ou...  31.3 us
    all_to_all x1, blocking collectives, shards(): packed = lax.all_to_all(packed, ('gx', 'gy'), 0, 0)  22.8 us
    all_to_all x1, blocking collectives, shards(): mixed = lax.all_to_all(mixed, ('gx', 'gy'), 0, 0)  19.7 us
    all_to_all x1, blocking collectives, shards(): gram = lax.all_to_all(gram, ('gx', 'gy', 'gz'), 0, 0)  10.3 us
    ppermute x2, waiting for transfers between devices, to_slab(): return lax.ppermute(x, ('gx', 'gz'), perm)  7 us
    ppermute x2, starting transfers between devices, to_slab(): return lax.ppermute(x, ('gx', 'gz'), perm)  3.76 us
  transfers between devices with their start and end apart: 2, of which 2 were waited for; matrix products, arithmetic and copies ran while one was open for 0% of the time, Pallas kernels for 0%

profile of v1, /device:TPU:0, one launch (start us, length us, event | category | flops | bytes accessed | tf_op | source)
XLA Modules:
  0.0 96.2 jit_solution(9875905135995239490)
XLA Ops:
  0.6 1.9 %pack.1 = f32[8,2,64,128]{3,2,1,0:T(8,128)} custom-call(f32[3,8,16,128]{3,2,1,0:T(8,128)} %f_ref.1, f32[8,16,128]{2,1,0:T(8,128)} %v_ref.1), custom_call_target="tpu_custom_call" | custom-call | tf_op jit(solution)/shard_map/pack/pallas_call | solution.py:389
  2.5 22.8 %all_to_all.15.in_ref = f32[8,2,64,128]{3,2,1,0:T(8,128)} all-to-all(f32[8,2,64,128]{3,2,1,0:T(8,128)} %pack.1), channel_id=1, replica_groups=mesh['gx'=2,'gy'=4,'gz'=4] {'gx','gy'}, dimensions={0} | all-to-all | bytes 1048576 | tf_op jit(solution)/shard_map/all_to_all | solution.py:407
  25.3 3.6 %planes.1 = (f32[2,64,8,128]{3,2,1,0:T(8,128)}, f32[2,30,8,128]{3,2,1,0:T(8,128)}, f32[2,30,8,128]{3,2,1,0:T(8,128)}) custom-call(f32[8,2,64,128]{3,2,1,0:T(8,128)} %all_to_all.15.in_ref), custom_call_target="tpu_custom_call" | custom-call | tf_op jit(solution)/shard_map/planes/pallas_call | solution.py:389
  28.9 2.5 %collective-permute-start = (f32[2,30,8,128]{3,2,1,0:T(8,128)}, f32[2,30,8,128]{3,2,1,0:T(8,128)S(1)}, u32[]{:S(2)}, u32[]{:S(2)}) collective-permute-start(f32[2,30,8,128]{3,2,1,0:T(8,128)} %get-tuple-element.9), channel_id=1, source_target_pairs={{0,16},{16,17},{17,1},{1,2},{2,18},{18,19},{19,3},{4,20},{20,21},{... | collective-permute-start | bytes 737288 | tf_op jit(solution)/shard_map/ppermute | solution.py:85
  31.4 1.3 %collective-permute-start.1 = (f32[2,30,8,128]{3,2,1,0:T(8,128)}, f32[2,30,8,128]{3,2,1,0:T(8,128)S(1)}, u32[]{:S(2)}, u32[]{:S(2)}) collective-permute-start(f32[2,30,8,128]{3,2,1,0:T(8,128)} %get-tuple-element.10), channel_id=1, source_target_pairs={{16,0},{17,16},{1,17},{2,1},{18,2},{19,18},{3,19},{20,4},{21,20},{... | collective-permute-start | bytes 737288 | tf_op jit(solution)/shard_map/ppermute | solution.py:85
  32.7 3.0 %collective-permute-done.refs_1_ = f32[2,30,8,128]{3,2,1,0:T(8,128)S(1)} collective-permute-done((f32[2,30,8,128]{3,2,1,0:T(8,128)}, f32[2,30,8,128]{3,2,1,0:T(8,128)S(1)}, u32[]{:S(2)}, u32[]{:S(2)}) %collective-permute-start) | collective-permute-done | bytes 245792 | tf_op jit(solution)/shard_map/ppermute | solution.py:85
  35.7 0.0 copy-start
  35.7 4.0 %collective-permute-done.1.refs_2_ = f32[2,30,8,128]{3,2,1,0:T(8,128)S(1)} collective-permute-done((f32[2,30,8,128]{3,2,1,0:T(8,128)}, f32[2,30,8,128]{3,2,1,0:T(8,128)S(1)}, u32[]{:S(2)}, u32[]{:S(2)}) %collective-permute-start.1) | collective-permute-done | bytes 245792 | tf_op jit(solution)/shard_map/ppermute | solution.py:85
  39.7 0.0 copy-start.1
  39.7 0.0 copy-done
  39.7 0.7 copy-done.1
  40.4 19.7 %basis.1 = (f32[3,64,8,128]{3,2,1,0:T(8,128)}, f32[3,64,8,128]{3,2,1,0:T(8,128)}, f32[32,1,128]{2,1,0:T(1,128)}) custom-call(f32[2,64,8,128]{3,2,1,0:T(8,128)} %get-tuple-element.8.refs_0_.main_ref, f32[2,30,8,128]{3,2,1,0:T(8,128)} %copy-done, f32[2,30,8,128]{3,2,1,0:T(8,128)} %copy-done.1), custom_call_target="tpu_custom_call" | custom-call | tf_op jit(solution)/shard_map/basis/pallas_call | solution.py:389
  60.1 10.3 %all_to_all.16.gram_ref = f32[32,1,128]{2,1,0:T(1,128)} all-to-all(f32[32,1,128]{2,1,0:T(1,128)} %get-tuple-element.11), channel_id=1, replica_groups=mesh['gx'=2,'gy'=4,'gz'=4] {'gx','gy','gz'}, dimensions={0} | all-to-all | bytes 32768 | tf_op jit(solution)/shard_map/all_to_all | solution.py:426
  70.4 4.2 %combine.1 = f32[8,2,64,128]{3,2,1,0:T(8,128)} custom-call(f32[32,1,128]{2,1,0:T(1,128)} %all_to_all.16.gram_ref, f32[2,64,8,128]{3,2,1,0:T(8,128)} %get-tuple-element.8.refs_0_.main_ref, f32[3,64,8,128]{3,2,1,0:T(8,128)} %get-tuple-element.12.u_ref, f32[3,64,8,128]{3,2,1,0:T(8,128)} %get-tuple-element.13.rho_ref), custom_call_target="tpu_custom_call" | custom-call | tf_op jit(solution)/shard_map/combine/pallas_call | solution.py:389
  74.6 19.7 %all_to_all.17.in_ref = f32[8,2,64,128]{3,2,1,0:T(8,128)} all-to-all(f32[8,2,64,128]{3,2,1,0:T(8,128)} %combine.1), channel_id=1, replica_groups=mesh['gx'=2,'gy'=4,'gz'=4] {'gx','gy'}, dimensions={0} | all-to-all | bytes 1048576 | tf_op jit(solution)/shard_map/all_to_all | solution.py:430
  94.3 1.9 %unpack.1 = (f32[3,8,16,128]{3,2,1,0:T(8,128)}, f32[3,8,16,128]{3,2,1,0:T(8,128)}) custom-call(f32[8,2,64,128]{3,2,1,0:T(8,128)} %all_to_all.17.in_ref), custom_call_target="tpu_custom_call" | custom-call | tf_op jit(solution)/shard_map/unpack/pallas_call | solution.py:389
Async XLA Ops:
  28.9 6.8 %collective-permute-start = (f32[2,30,8,128]{3,2,1,0:T(8,128)}, f32[2,30,8,128]{3,2,1,0:T(8,128)S(1)}, u32[]{:S(2)}, u32[]{:S(2)}) collective-permute-start(f32[2,30,8,128]{3,2,1,0:T(8,128)} %get-tuple-element.9), channel_id=1, source_target_pairs={{0,16},{16,17},{17,1},{1,2},{2,18},{18,19},{19,3},{4,20},{20,21},{... | collective-permute-start | bytes 737288 | tf_op jit(solution)/shard_map/ppermute | solution.py:85
  31.4 8.3 %collective-permute-start.1 = (f32[2,30,8,128]{3,2,1,0:T(8,128)}, f32[2,30,8,128]{3,2,1,0:T(8,128)S(1)}, u32[]{:S(2)}, u32[]{:S(2)}) collective-permute-start(f32[2,30,8,128]{3,2,1,0:T(8,128)} %get-tuple-element.10), channel_id=1, source_target_pairs={{16,0},{17,16},{1,17},{2,1},{18,2},{19,18},{3,19},{20,4},{21,20},{... | collective-permute-start | bytes 737288 | tf_op jit(solution)/shard_map/ppermute | solution.py:85
  35.7 4.0 %copy-start = (f32[2,30,8,128]{3,2,1,0:T(8,128)}, f32[2,30,8,128]{3,2,1,0:T(8,128)S(1)}, u32[]{:S(2)}) copy-start(f32[2,30,8,128]{3,2,1,0:T(8,128)S(1)} %collective-permute-done.refs_1_) | copy-start | bytes 737284
  39.7 0.7 copy-start.1

commit v2 on v1

--- a/solution.py
+++ b/solution.py
@@ -1,4 +1,5 @@
 import functools
+import math
 import jax
 import jax.numpy as jnp
 from jax import lax
@@ -13,7 +14,7 @@
 
 STEP = 2 * (CSWEEPS - 1) + 4
 HALO = ITERS * STEP
-CHUNK = 16
+BLOCK_ROWS = 1024
 
 
 def lane_iota(shape):
@@ -65,6 +66,7 @@
         self.width = self.gy * yl
         self.lanes = xl * yl
         self.window = self.planes + 2 * HALO
+        self.chunk = max(2, BLOCK_ROWS // self.rows)
         self.hops = []
         left = HALO
         while left > 0:
@@ -120,7 +122,7 @@
             v = scr[pl.ds(rows, n * sz.group), :].reshape(n, sz.group, sz.lanes)
             main_ref[a, pl.ds(p, n)] = swap_blocks(v, sz.gy, sz.yl)
 
-        chunked(0, sz.planes, CHUNK, body)
+        chunked(0, sz.planes, sz.chunk, body)
         k = 0
         for count in sz.hops:
             if count < sz.planes:
@@ -140,7 +142,7 @@
     rhos = [next(it) for _ in range(ITERS + 1)]
     us = [next(it) for _ in range(ITERS)]
 
-    H, N, W = HALO, sz.planes, sz.window
+    H, N, W, C = HALO, sz.planes, sz.window, sz.chunk
     for a, ref in ((0, rhos[0]), (1, visc)):
         ref[H : H + N] = main_ref[a]
         at_lo, at_hi = H, H + N
@@ -171,7 +173,7 @@
     def fine_faces(p, n):
         cz[pl.ds(p, n)] = faces_z(visc, p, n, 0.5)
 
-    chunked(0, W - 1, CHUNK, fine_faces)
+    chunked(0, W - 1, C, fine_faces)
 
     def fine_coeffs(p, n):
         v = visc[pl.ds(p, n)]
@@ -191,7 +193,7 @@
         mass[pl.ds(p, n)] = m
         od[pl.ds(p, n)] = RELAX / (m + inner + outer + yp + ym + cz[pl.ds(p - 1, n)] + cz[pl.ds(p, n)])
 
-    chunked(1, W - 1, CHUNK, fine_coeffs)
+    chunked(1, W - 1, C, fine_coeffs)
 
     def gather_block(fine, n):
         t = fine.reshape(n, 2, sz.rows, sz.lanes)
@@ -202,12 +204,12 @@
     def coarse_visc(p, n):
         cv[pl.ds(p, n)] = 0.125 * gather_block(visc[pl.ds(2 * p, 2 * n)], n)
 
-    chunked(0, W // 2, CHUNK // 2, coarse_visc)
+    chunked(0, W // 2, C // 2, coarse_visc)
 
     def coarse_faces(p, n):
         ccz[pl.ds(p, n)] = faces_z(cv, p, n, 2.0)
 
-    chunked(0, W // 2 - 1, CHUNK, coarse_faces)
+    chunked(0, W // 2 - 1, C, coarse_faces)
     cedge_yp, cedge_ym = y >= sz.width - 2, y < 2
 
     def coarse_coeffs(p, n):
@@ -226,7 +228,7 @@
         cmass[pl.ds(p, n)] = m
         cod[pl.ds(p, n)] = RELAX / (m + xp + roll(xp, 1, 1) + yp + ym + ccz[pl.ds(p - 1, n)] + ccz[pl.ds(p, n)])
 
-    chunked(1, W // 2 - 1, CHUNK, coarse_coeffs)
+    chunked(1, W // 2 - 1, C, coarse_coeffs)
 
     def fine_apply(ref, p, n):
         ext = ref[pl.ds(p - 1, n + 2)]
@@ -255,7 +257,7 @@
         def smooth(p, n):
             sm[pl.ds(p, n)] = od[pl.ds(p, n)] * rho[pl.ds(p, n)]
 
-        spread(reach, CHUNK, smooth)
+        spread(reach, C, smooth)
 
         def restricted(p, n):
             defect = rho[pl.ds(2 * p, 2 * n)] - fine_apply(sm, 2 * p, 2 * n)
@@ -263,7 +265,7 @@
             rhs[pl.ds(p, n)] = b
             c0[pl.ds(p, n)] = cod[pl.ds(p, n)] * b
 
-        spread(reach - 1, CHUNK // 2, restricted, 2)
+        spread(reach - 1, C // 2, restricted, 2)
         old, new = c0, c1
         for sweep in range(1, CSWEEPS):
 
@@ -271,7 +273,7 @@
                 at = pl.ds(p, n)
                 new[at] = old[at] + cod[at] * (rhs[at] - coarse_apply(old, p, n))
 
-            spread(reach - 1 - 2 * sweep, CHUNK, relax, 2)
+            spread(reach - 1 - 2 * sweep, C, relax, 2)
             old, new = new, old
         reach = reach - 1 - 2 * (CSWEEPS - 1)
 
@@ -280,18 +282,18 @@
             fine = jnp.stack([c, c], axis=1).reshape(2 * n, sz.rows, sz.lanes)
             sm2[pl.ds(2 * p, 2 * n)] = sm[pl.ds(2 * p, 2 * n)] + fine
 
-        spread(reach, CHUNK // 2, prolonged, 2)
+        spread(reach, C // 2, prolonged, 2)
 
         def smoothed(p, n):
             at = pl.ds(p, n)
             u[at] = sm2[at] + od[at] * (rho[at] - fine_apply(sm2, p, n))
 
-        spread(reach - 1, CHUNK, smoothed)
+        spread(reach - 1, C, smoothed)
 
         def descend(p, n):
             rho_next[pl.ds(p, n)] = rho[pl.ds(p, n)] - fine_apply(u, p, n)
 
-        spread(reach - 2, CHUNK, descend)
+        spread(reach - 2, C, descend)
 
     pairs = [(j, k) for j in range(ITERS + 1) for k in range(ITERS)]
 
@@ -366,7 +368,7 @@
             rows = pl.multiple_of(p * sz.group, 8)
             scr[pl.ds(rows, n * sz.group), :] = v.reshape(n * sz.group, sz.lanes)
 
-        chunked(0, sz.planes, CHUNK, body)
+        chunked(0, sz.planes, sz.chunk, body)
         for dest in range(sz.group):
             out_ref[dest, a] = scr[pl.ds(dest, sz.planes, stride=sz.group), :]
 
@@ -386,13 +388,14 @@
 
 def call(kernel, sz, ins, outs, scratch=(), name=None):
     outs = [jax.ShapeDtypeStruct(s, jnp.float32) for s in outs]
+    held = sum(math.prod(s) for s in [a.shape for a in ins] + [o.shape for o in outs] + list(scratch))
     return pl.pallas_call(
         functools.partial(kernel, sz),
         in_specs=vmem(len(ins)),
         out_specs=vmem(len(outs)),
         out_shape=outs,
         scratch_shapes=[pltpu.VMEM(s, jnp.float32) for s in scratch],
-        compiler_params=pltpu.CompilerParams(vmem_limit_bytes=56 * 2**20),
+        compiler_params=pltpu.CompilerParams(vmem_limit_bytes=4 * held + 3 * 2**20),
         name=name,
     )(*ins)
 

time: 96.7 us -> 72 us (0.74)
  Pallas kernels: 31.3 us -> 9.19 us
  blocking collectives: 52.8 us -> 49.5 us
  local copies, waits for them, and re-layouts: 0.68 us -> 1.76 us
    pallas_call x5, Pallas kernels: 31.3 us -> 9.19 us  [call(): pl.pallas_call(functools.partial(kernel, sz), in_specs=vmem(len(ins)), ou...]
    all_to_all x1, blocking collectives: 19.7 us -> 18.1 us  [shards(): mixed = lax.all_to_all(mixed, ('gx', 'gy'), 0, 0)]
    all_to_all x1, blocking collectives: 10.3 us -> 8.88 us  [shards(): gram = lax.all_to_all(gram, ('gx', 'gy', 'gz'), 0, 0)]
    unnamed x4, local copies, waits for them, and re-layouts: 0.68 us -> 1.76 us
where the time goes in v2:
time: 72 us; the launch traced here: 71.7 us
  blocking collectives  49.5 us (69%)
  Pallas kernels  9.19 us (13%)
  waiting for transfers between devices  6.79 us (9%)
  starting transfers between devices  3.77 us (5%)
  local copies, waits for them, and re-layouts  1.76 us (2%)
    all_to_all x1, blocking collectives, shards(): packed = lax.all_to_all(packed, ('gx', 'gy'), 0, 0)  22.5 us
    all_to_all x1, blocking collectives, shards(): mixed = lax.all_to_all(mixed, ('gx', 'gy'), 0, 0)  18.1 us
    pallas_call x5, Pallas kernels, call(): pl.pallas_call(functools.partial(kernel, sz), in_specs=vmem(len(ins)), ou...  9.19 us
    all_to_all x1, blocking collectives, shards(): gram = lax.all_to_all(gram, ('gx', 'gy', 'gz'), 0, 0)  8.88 us
    ppermute x2, waiting for transfers between devices, to_slab(): return lax.ppermute(x, ('gx', 'gz'), perm)  6.79 us
    ppermute x2, starting transfers between devices, to_slab(): return lax.ppermute(x, ('gx', 'gz'), perm)  3.77 us
    unnamed x4, local copies, waits for them, and re-layouts  1.76 us
  transfers between devices with their start and end apart: 2, of which 2 were waited for; matrix products, arithmetic and copies ran while one was open for 0% of the time, Pallas kernels for 0%

profile of v2, /device:TPU:0, one launch (start us, length us, event | category | flops | bytes accessed | tf_op | source)
XLA Modules:
  0.0 71.7 jit_solution(15006275697516501346)
XLA Ops:
  0.6 0.0 copy-start
  0.6 0.9 %copy-done = f32[3,8,16,128]{3,2,1,0:T(8,128)S(1)} copy-done((f32[3,8,16,128]{3,2,1,0:T(8,128)S(1)}, f32[3,8,16,128]{3,2,1,0:T(8,128)}, u32[]{:S(2)}) %copy-start) | copy-done | bytes 196632
  1.6 0.0 copy-start.1
  1.6 0.8 %copy-done.1 = f32[8,16,128]{2,1,0:T(8,128)S(1)} copy-done((f32[8,16,128]{2,1,0:T(8,128)S(1)}, f32[8,16,128]{2,1,0:T(8,128)}, u32[]{:S(2)}) %copy-start.1) | copy-done | bytes 65560
  2.4 0.1 pack.1
  2.5 22.5 %all_to_all.15.in_ref = f32[8,2,64,128]{3,2,1,0:T(8,128)S(1)} all-to-all(f32[8,2,64,128]{3,2,1,0:T(8,128)S(1)} %pack.1), channel_id=1, replica_groups=mesh['gx'=2,'gy'=4,'gz'=4] {'gx','gy'}, dimensions={0} | all-to-all | bytes 1048576 | tf_op jit(solution)/shard_map/all_to_all | solution.py:410
  25.0 0.6 planes.1
  25.7 2.5 %collective-permute-start = (f32[2,30,8,128]{3,2,1,0:T(8,128)S(1)}, f32[2,30,8,128]{3,2,1,0:T(8,128)S(1)}, u32[]{:S(2)}, u32[]{:S(2)}) collective-permute-start(f32[2,30,8,128]{3,2,1,0:T(8,128)S(1)} %get-tuple-element.9), channel_id=1, source_target_pairs={{0,16},{16,17},{17,1},{1,2},{2,18},{18,19},{19,3},{4,20},{20,21},{... | collective-permute-start | bytes 737288 | tf_op jit(solution)/shard_map/ppermute | solution.py:87
  28.2 1.3 %collective-permute-start.1 = (f32[2,30,8,128]{3,2,1,0:T(8,128)S(1)}, f32[2,30,8,128]{3,2,1,0:T(8,128)S(1)}, u32[]{:S(2)}, u32[]{:S(2)}) collective-permute-start(f32[2,30,8,128]{3,2,1,0:T(8,128)S(1)} %get-tuple-element.10), channel_id=1, source_target_pairs={{16,0},{17,16},{1,17},{2,1},{18,2},{19,18},{3,19},{20,4},{21,20},{... | collective-permute-start | bytes 737288 | tf_op jit(solution)/shard_map/ppermute | solution.py:87
  29.5 2.7 %collective-permute-done.refs_1_ = f32[2,30,8,128]{3,2,1,0:T(8,128)S(1)} collective-permute-done((f32[2,30,8,128]{3,2,1,0:T(8,128)S(1)}, f32[2,30,8,128]{3,2,1,0:T(8,128)S(1)}, u32[]{:S(2)}, u32[]{:S(2)}) %collective-permute-start) | collective-permute-done | bytes 245792 | tf_op jit(solution)/shard_map/ppermute | solution.py:87
  32.2 4.1 %collective-permute-done.1.refs_2_ = f32[2,30,8,128]{3,2,1,0:T(8,128)S(1)} collective-permute-done((f32[2,30,8,128]{3,2,1,0:T(8,128)S(1)}, f32[2,30,8,128]{3,2,1,0:T(8,128)S(1)}, u32[]{:S(2)}, u32[]{:S(2)}) %collective-permute-start.1) | collective-permute-done | bytes 245792 | tf_op jit(solution)/shard_map/ppermute | solution.py:87
  36.2 6.7 %basis.1 = (f32[3,64,8,128]{3,2,1,0:T(8,128)S(1)}, f32[3,64,8,128]{3,2,1,0:T(8,128)S(1)}, f32[32,1,128]{2,1,0:T(1,128)S(1)}) custom-call(f32[2,64,8,128]{3,2,1,0:T(8,128)S(1)} %get-tuple-element.8.refs_0_.main_ref, f32[2,30,8,128]{3,2,1,0:T(8,128)S(1)} %collective-permute-done.refs_1_, f32[2,30,8,128]{3,2,1,0:T(8,128)S(1)} %collective-permute-done.1.refs_2_), custom_call_target="tpu_custom_call" | custom-call | tf_op jit(solution)/shard_map/basis/pallas_call | solution.py:392
  43.0 8.9 %all_to_all.16.gram_ref = f32[32,1,128]{2,1,0:T(1,128)S(1)} all-to-all(f32[32,1,128]{2,1,0:T(1,128)S(1)} %get-tuple-element.11), channel_id=1, replica_groups=mesh['gx'=2,'gy'=4,'gz'=4] {'gx','gy','gz'}, dimensions={0} | all-to-all | bytes 32768 | tf_op jit(solution)/shard_map/all_to_all | solution.py:429
  51.8 0.9 %combine.1 = f32[8,2,64,128]{3,2,1,0:T(8,128)S(1)} custom-call(f32[32,1,128]{2,1,0:T(1,128)S(1)} %all_to_all.16.gram_ref, f32[2,64,8,128]{3,2,1,0:T(8,128)S(1)} %get-tuple-element.8.refs_0_.main_ref, f32[3,64,8,128]{3,2,1,0:T(8,128)S(1)} %get-tuple-element.12.u_ref, f32[3,64,8,128]{3,2,1,0:T(8,128)S(1)} %get-tuple-element.13.rho_ref), custom_call_target="tpu_custom_call" | custom-call | tf_op jit(solution)/shard_map/combine/pallas_call | solution.py:392
  52.7 18.1 %all_to_all.17.in_ref = f32[8,2,64,128]{3,2,1,0:T(8,128)S(1)} all-to-all(f32[8,2,64,128]{3,2,1,0:T(8,128)S(1)} %combine.1), channel_id=1, replica_groups=mesh['gx'=2,'gy'=4,'gz'=4] {'gx','gy'}, dimensions={0} | all-to-all | bytes 1048576 | tf_op jit(solution)/shard_map/all_to_all | solution.py:433
  70.8 0.9 %unpack.1 = (f32[3,8,16,128]{3,2,1,0:T(8,128)}, f32[3,8,16,128]{3,2,1,0:T(8,128)}) custom-call(f32[8,2,64,128]{3,2,1,0:T(8,128)S(1)} %all_to_all.17.in_ref), custom_call_target="tpu_custom_call" | custom-call | tf_op jit(solution)/shard_map/unpack/pallas_call | solution.py:392
Async XLA Ops:
  0.6 0.9 %copy-start = (f32[3,8,16,128]{3,2,1,0:T(8,128)S(1)}, f32[3,8,16,128]{3,2,1,0:T(8,128)}, u32[]{:S(2)}) copy-start(f32[3,8,16,128]{3,2,1,0:T(8,128)} %f_ref.1) | copy-start | bytes 589828
  1.6 0.8 %copy-start.1 = (f32[8,16,128]{2,1,0:T(8,128)S(1)}, f32[8,16,128]{2,1,0:T(8,128)}, u32[]{:S(2)}) copy-start(f32[8,16,128]{2,1,0:T(8,128)} %v_ref.1) | copy-start | bytes 196612
  25.7 6.5 %collective-permute-start = (f32[2,30,8,128]{3,2,1,0:T(8,128)S(1)}, f32[2,30,8,128]{3,2,1,0:T(8,128)S(1)}, u32[]{:S(2)}, u32[]{:S(2)}) collective-permute-start(f32[2,30,8,128]{3,2,1,0:T(8,128)S(1)} %get-tuple-element.9), channel_id=1, source_target_pairs={{0,16},{16,17},{17,1},{1,2},{2,18},{18,19},{19,3},{4,20},{20,21},{... | collective-permute-start | bytes 737288 | tf_op jit(solution)/shard_map/ppermute | solution.py:87
  28.2 8.1 %collective-permute-start.1 = (f32[2,30,8,128]{3,2,1,0:T(8,128)S(1)}, f32[2,30,8,128]{3,2,1,0:T(8,128)S(1)}, u32[]{:S(2)}, u32[]{:S(2)}) collective-permute-start(f32[2,30,8,128]{3,2,1,0:T(8,128)S(1)} %get-tuple-element.10), channel_id=1, source_target_pairs={{16,0},{17,16},{1,17},{2,1},{18,2},{19,18},{3,19},{20,4},{21,20},{... | collective-permute-start | bytes 737288 | tf_op jit(solution)/shard_map/ppermute | solution.py:87

commit v3 on v2

v3 whole, which is shorter than its diff:
```python
import functools
import math
import jax
import jax.numpy as jnp
from jax import lax
from jax.experimental import pallas as pl
from jax.experimental.pallas import tpu as pltpu
from jax.sharding import PartitionSpec as P

ITERS = 3
CSWEEPS = 4
REACTION = 1.0
RELAX = 2.0 / 3.0

STEP = 2 * (CSWEEPS - 1) + 4
HALO = ITERS * STEP
BLOCK_ROWS = 1024
STATE_LIMIT = 6 * 2**20


def lane_iota(shape):
    return lax.broadcasted_iota(jnp.int32, shape, len(shape) - 1)


def sub_iota(shape):
    return lax.broadcasted_iota(jnp.int32, shape, len(shape) - 2)


def roll(v, shift, dim):
    size = v.shape[dim]
    return pltpu.roll(v, shift % size, dim)


def swap_blocks(v, count, width):
    sub, lane = sub_iota(v.shape), lane_iota(v.shape)
    step = 1
    while step < count:
        low = (sub // step) % 2 == 1
        high = (lane // (step * width)) % 2 == 1
        rows, lanes = v.ndim - 2, v.ndim - 1
        from_left = roll(roll(v, step, rows), -step * width, lanes)
        from_right = roll(roll(v, -step, rows), step * width, lanes)
        v = jnp.where(low == high, v, jnp.where(low, from_left, from_right))
        step *= 2
    return v


def chunked(lo, hi, n, body):
    n = min(n, hi - lo)
    count = -(-(hi - lo) // n)
    if count == 1:
        body(lo, n)
        return

    @pl.loop(0, count)
    def _(i):
        body(jnp.minimum(lo + i * n, hi - n), n)


class Sizes:
    def __init__(self, mesh, comps, xl, yl, zl):
        self.gx, self.gy, self.gz = (mesh[a] for a in ("gx", "gy", "gz"))
        self.comps, self.xl, self.yl, self.zl = comps, xl, yl, zl
        self.group = self.gx * self.gy
        self.planes = zl // self.gx
        self.rows = self.gx * xl // 2
        self.width = self.gy * yl
        self.lanes = xl * yl
        self.window = self.planes + 2 * HALO
        self.chunk = max(2, BLOCK_ROWS // self.rows)
        self.hops = []
        left = HALO
        while left > 0:
            self.hops.append(min(left, self.planes))
            left -= self.planes
        self.paired = len(self.hops) == 1 and HALO < self.planes
        assert comps <= self.gy and xl == 2 * self.gy
        assert zl % self.gx == 0 and self.planes % 2 == 0 and self.window % 4 == 0 and 2 * self.width == self.lanes


def slab_of(sz, i):
    z, k = divmod(i, sz.gx)
    return (k if z % 2 == 0 else sz.gx - 1 - k) * sz.gz + z


def to_slab(sz, x, moves):
    n = sz.gx * sz.gz
    perm = [(slab_of(sz, i), slab_of(sz, j)) for i, j in moves(n) if 0 <= j < n]
    return lax.ppermute(x, ("gx", "gz"), perm)


def shifted(x, sz, by):
    return to_slab(sz, x, lambda n: [(i, i + by) for i in range(n)])


def swapped_pairs(x, sz, first):
    return to_slab(sz, x, lambda n: [(i, i + 1 if (i - first) % 2 == 0 else i - 1) for i in range(n)])


def odd_slab(sz):
    place = lax.axis_index("gx")
    line = lax.axis_index("gz")
    place = jnp.where(line % 2 == 1, sz.gx - 1 - place, place)
    return (line * sz.gx + place) % 2 == 1


def x_order(sz):
    return list(range(0, sz.xl, 2)) + list(range(1, sz.xl, 2))


def part_of(sz, half):
    odd = lax.axis_index("gz") % 2
    return jnp.where(odd == 1, sz.gx - 1 - half, half)


def pack_kernel(sz, f_hbm, v_hbm, out_ref, f_ref, v_ref, sems):
    copies = [pltpu.make_async_copy(v_hbm, v_ref, sems.at[0])]
    copies += [pltpu.make_async_copy(f_hbm.at[c], f_ref.at[c], sems.at[1 + c]) for c in range(sz.comps)]
    for copy in copies:
        copy.start()

    def turned(at):
        return jnp.concatenate([at(x) for x in x_order(sz)], axis=0).T

    def put(c, a, field):
        for half in range(sz.gx):
            out_ref[part_of(sz, half) * sz.gy + c, a] = field[half * sz.planes : (half + 1) * sz.planes]

    for c in range(sz.comps, sz.gy):
        for a in range(2):
            put(c, a, jnp.zeros((sz.zl, sz.lanes), jnp.float32))
    copies[0].wait()
    visc = turned(lambda x: v_ref[x])
    for c in range(sz.comps):
        put(c, 1, visc)
    for c in range(sz.comps):
        copies[1 + c].wait()
        put(c, 0, turned(lambda x: f_ref[c, x]))


def planes_kernel(sz, in_ref, main_ref, *rest):
    edges, scr = rest[:-1], rest[-1]
    for a in range(2):
        for src in range(sz.group):
            scr[pl.ds(src, sz.planes, stride=sz.group), :] = in_ref[src, a]

        def body(p, n):
            rows = pl.multiple_of(p * sz.group, 8)
            v = scr[pl.ds(rows, n * sz.group), :].reshape(n, sz.group, sz.lanes)
            main_ref[a, pl.ds(p, n)] = swap_blocks(v, sz.gy, sz.yl)

        chunked(0, sz.planes, sz.chunk, body)
        k = 0
        for count in sz.hops:
            if sz.paired:
                lo, hi = 0, sz.planes - count
                odd = odd_slab(sz)
                edges[0][a] = main_ref[a, pl.ds(jnp.where(odd, lo, hi), count)]
                edges[1][a] = main_ref[a, pl.ds(jnp.where(odd, hi, lo), count)]
            elif count < sz.planes:
                edges[k][a] = main_ref[a, 0:count]
                edges[k + 1][a] = main_ref[a, sz.planes - count : sz.planes]
                k += 2


FINE_ARRAYS = 14 + 3 * ITERS + ITERS + 1
COARSE_ARRAYS = 9 + ITERS * CSWEEPS


def basis_kernel(phase, sz, *refs):
    it = iter(refs)
    main_ref = next(it) if phase != 1 else None
    halos = [next(it) for _ in range(2 * len(sz.hops))] if phase != 0 else None
    if phase == 1:
        next(it), next(it)
    if phase == 1 or phase == 0:
        fine_state, coarse_state = next(it), next(it)
    u_out, rho_out, gram_out = (next(it) for _ in range(3)) if phase != 0 else (None,) * 3
    if phase is None:
        fine_state, coarse_state = next(it), next(it)
    it = iter([fine_state.at[i] for i in range(FINE_ARRAYS)])
    half, cin, cout, cyp, cym, cz, mass, od = (next(it) for _ in range(8))
    sin, sout, syp, sym, szp, szm = (next(it) for _ in range(6))
    sms, sm2s, us = ([next(it) for _ in range(ITERS)] for _ in range(3))
    rhos = [next(it) for _ in range(ITERS + 1)]
    it = iter([coarse_state.at[i] for i in range(COARSE_ARRAYS)])
    twice, ccz, cod, kxp, kxm, kyp, kym, kzp, kzm = (next(it) for _ in range(9))
    corrections = [[next(it) for _ in range(CSWEEPS)] for _ in range(ITERS)]

    H, N, W, C = HALO, sz.planes, sz.window, sz.chunk
    Q, QC = W // 2, W // 4

    def run(outer, inner, end, n, body, ref=None):
        cut = min(inner, end)
        lo, hi = {None: (outer, end), 0: (cut, end), 1: (outer, cut)}[phase]
        if lo < hi:
            chunked(lo, hi, n, body)
            if ref is not None and hi == end:
                ref[end] = roll(ref[end - 1], sz.width, ref.ndim - 2)

    plane = (1, sz.rows, sz.lanes)
    lane, sub = lane_iota(plane), sub_iota(plane)
    below = lane < sz.width
    y = lane % sz.width
    last = sub == sz.rows - 1

    def plane_at(a, p):
        if H <= p < H + N:
            return main_ref[a, p - H]
        if sz.paired:
            own, other = (halos[i][a, p if p < H else p - H - N] for i in (0, 1))
            return jnp.where(odd_slab(sz) == (p < H), own, other)
        lo, hi = H, H + N
        for j, count in enumerate(sz.hops):
            if lo - count <= p < lo:
                return halos[2 * j][a, p - lo + count]
            if hi <= p < hi + count:
                return halos[2 * j + 1][a, p - hi]
            lo, hi = lo - count, hi + count

    for a, ref in ((1, half), (0, rhos[0])):

        def place(q, n):
            p = jnp.stack([plane_at(a, q + i) for i in range(n)])
            m = jnp.stack([plane_at(a, W - 1 - q - i) for i in range(n)])
            if a == 1:
                p, m = 0.5 * p, 0.5 * m
            ref[q : q + n, 0] = jnp.where(below, p, roll(m, sz.width, 2))
            ref[q : q + n, 1] = jnp.where(below, roll(p, sz.width, 2), m)

        run(0, H, Q, Q, place, half if a == 1 else None)

    def count_of(*edges):
        return sum(e.astype(jnp.float32) for e in edges)

    def z_faces(cells, faces, inner, size):
        def body(q, n):
            faces[pl.ds(q, n)] = cells[pl.ds(q, n)] + cells[pl.ds(q + 1, n)]

        run(0, inner, size, C // 2, body)

    def close_z(cells, faces, first, step, mass_ref=None):
        if phase == 0:
            return
        for q in range(first, -1, -step):
            outside = ~((cells[q] > 0) & (cells[q + 1] > 0))
            total = faces[q]
            faces[q] = jnp.where(outside, 0.0, total)
            if mass_ref is not None:
                moved = jnp.where(outside, total, 0.0)
                for near in (q, q + 1):
                    if near > 0:
                        mass_ref[near] = mass_ref[near] + moved

    z_faces(half, cz, H, Q)
    edge_out = (sub == 0, last)
    edge_y = y == sz.width - 1

    def fine_coeffs(q, n):
        at, under = pl.ds(q, n), pl.ds(q - 1, n)
        h = [half[at, i] for i in (0, 1)]
        inner = h[0] + h[1]
        outer = [None, jnp.where(last, 0.0, h[1] + roll(h[0], -1, 1))]
        outer[0] = roll(outer[1], 1, 1)
        for i in (0, 1):
            yp = jnp.where(edge_y, 0.0, h[i] + roll(h[i], -1, 2))
            ym = roll(yp, 1, 2)
            m = REACTION + count_of(edge_out[i], edge_y, y == 0) * h[i]
            scale = RELAX / (m + inner + outer[i] + (yp + ym) + (cz[under, i] + cz[at, i]))
            cin[at, i], cout[at, i], cyp[at, i], cym[at, i] = inner, outer[i], yp, ym
            mass[at, i], od[at, i] = m, scale
            sin[at, i], sout[at, i], syp[at, i], sym[at, i] = scale * inner, scale * outer[i], scale * yp, scale * ym

    run(1, H + 1, Q, C // 2, fine_coeffs)
    close_z(half, cz, H - 1, N, mass)

    def fine_z(q, n):
        at = pl.ds(q, n)
        szp[at] = od[at] * cz[at]
        szm[at] = od[at] * cz[pl.ds(q - 1, n)]

    run(1, H + 1, Q, C // 2, fine_z)

    def gather_block(fine, n):
        t = fine.reshape(n, 2, sz.rows, sz.lanes)
        t = t[:, 0] + t[:, 1]
        return t + jnp.where(lane % 2 == 0, roll(t, -1, 2), roll(t, 1, 2))

    def coarse_visc(q, n):
        fine = pl.ds(2 * q, 2 * n)
        twice[pl.ds(q, n)] = 0.5 * gather_block(half[fine, 0] + half[fine, 1], n)

    run(0, H // 2, QC, C // 4, coarse_visc, twice)
    z_faces(twice, ccz, H // 2, QC)
    edge_y2 = y >= sz.width - 2
    outer_coarse = count_of(sub == 0, last, edge_y2, y < 2)

    def coarse_coeffs(q, n):
        at = pl.ds(q, n)
        t = twice[at]
        xp = jnp.where(last, 0.0, t + roll(t, -1, 1))
        yp = jnp.where(edge_y2, 0.0, t + roll(t, -2, 2))
        xm, ym = roll(xp, 1, 1), roll(yp, 2, 2)
        m = 8.0 * REACTION + outer_coarse * t
        scale = RELAX / (m + (xp + xm) + (yp + ym) + (ccz[pl.ds(q - 1, n)] + ccz[at]))
        cod[at] = scale
        kxp[at], kxm[at], kyp[at], kym[at] = scale * xp, scale * xm, scale * yp, scale * ym

    run(1, H // 2 + 1, QC, C // 2, coarse_coeffs)
    close_z(twice, ccz, H // 2 - 1, N // 2)

    def coarse_z(q, n):
        at = pl.ds(q, n)
        kzp[at] = cod[at] * ccz[at]
        kzm[at] = cod[at] * ccz[pl.ds(q - 1, n)]

    run(1, H // 2 + 1, QC, C // 2, coarse_z)

    def fine_beside(ref, q, n, coeffs):
        at, under, over = pl.ds(q, n), pl.ds(q - 1, n), pl.ds(q + 1, n)
        inner, outer, yp, ym, z_over, z_under = coeffs
        out = []
        for i in (0, 1):
            v, w = ref[at, i], ref[at, 1 - i]
            total = inner[at, i] * w + outer[at, i] * roll(w, -1 if i else 1, 1)
            total = total + (z_over(at, under, i) * ref[over, i] + z_under(at, under, i) * ref[under, i])
            out.append(total + (yp[at, i] * roll(v, -1, 2) + ym[at, i] * roll(v, 1, 2)))
        return out

    plain = (cin, cout, cyp, cym, lambda at, under, i: cz[at, i], lambda at, under, i: cz[under, i])
    scaled = (sin, sout, syp, sym, lambda at, under, i: szp[at, i], lambda at, under, i: szm[at, i])

    def fine_apply(ref, q, n):
        at = pl.ds(q, n)
        v = [ref[at, i] for i in (0, 1)]
        fin = cin[at, 0] * (v[0] - v[1])
        fout = cout[at, 1] * (v[1] - roll(v[0], -1, 1))
        fx = (fin - roll(fout, 1, 1), fout - fin)
        out = []
        for i in (0, 1):
            ext = ref[pl.ds(q - 1, n + 2), i]
            flux = cz[pl.ds(q - 1, n + 1), i] * (ext[: n + 1] - ext[1:])
            fy = cyp[at, i] * (v[i] - roll(v[i], -1, 2))
            out.append(mass[at, i] * v[i] + (flux[1:] - flux[:n]) + (fy - roll(fy, 1, 2)) + fx[i])
        return out

    known = H
    for k in range(ITERS):
        outer = H - (HALO - 1 - k * STEP)
        rho, rho_next, u, sm, sm2 = rhos[k], rhos[k + 1], us[k], sms[k], sm2s[k]

        def smooth(q, n):
            sm[pl.ds(q, n)] = od[pl.ds(q, n)] * rho[pl.ds(q, n)]

        known = max(known, H + 1)
        run(outer, known, Q, C // 2, smooth, sm)

        first = corrections[k][0]

        def restricted(q, n):
            fine = pl.ds(2 * q, 2 * n)
            left, right = fine_beside(sm, 2 * q, 2 * n, plain)
            defect = (1.0 - RELAX) * (rho[fine, 0] + rho[fine, 1]) + (left + right)
            first[pl.ds(q, n)] = cod[pl.ds(q, n)] * gather_block(defect, n)

        outer, known = (outer + 1) // 2, (known + 2) // 2
        run(outer, known, QC, C // 4, restricted, first)
        for old, new in zip(corrections[k], corrections[k][1:]):

            def relax(q, n):
                at = pl.ds(q, n)
                v = old[at]
                total = first[at] + (1.0 - RELAX) * v
                total = total + (kzp[at] * old[pl.ds(q + 1, n)] + kzm[at] * old[pl.ds(q - 1, n)])
                total = total + (kxp[at] * roll(v, -1, 1) + kxm[at] * roll(v, 1, 1))
                new[at] = total + (kyp[at] * roll(v, -2, 2) + kym[at] * roll(v, 2, 2))

            outer, known = outer + 1, known + 1
            run(outer, known, QC, C // 2, relax, new)

        def prolonged(q, n):
            c = new[pl.ds(q, n)]
            fine = jnp.stack([c, c], axis=1).reshape(2 * n, sz.rows, sz.lanes)
            for i in (0, 1):
                sm2[pl.ds(2 * q, 2 * n), i] = sm[pl.ds(2 * q, 2 * n), i] + fine

        run(outer, known, QC, C // 4, prolonged)
        if phase is None or phase == (0 if known < QC else 1):
            sm2[Q] = roll(sm2[Q - 1], sz.width, 2)

        def smoothed(q, n):
            at = pl.ds(q, n)
            for i, beside in enumerate(fine_beside(sm2, q, n, scaled)):
                u[at, i] = (1.0 - RELAX) * sm2[at, i] + sm[at, i] + beside

        outer, known = 2 * outer + 1, 2 * known + 1
        run(outer, known, Q, C // 2, smoothed, u)

        def descend(q, n):
            at = pl.ds(q, n)
            for i, image in enumerate(fine_apply(u, q, n)):
                rho_next[at, i] = rho[at, i] - image

        outer, known = outer + 1, known + 1
        run(outer, known, Q, C // 2, descend)

    if phase == 0:
        return
    pairs = [(j, k) for j in range(ITERS + 1) for k in range(ITERS)]

    def products(q, sums):
        for i in (0, 1):
            rv = [r[H + q, i] for r in rhos]
            uv = [u[H + q, i] for u in us]
            for k in range(ITERS):
                u_out[k, q, i] = uv[k]
            for j in range(ITERS + 1):
                rho_out[j, q, i] = rv[j]
            sums = tuple(s + rv[j] * uv[k] for s, (j, k) in zip(sums, pairs))
        return sums

    zero = jnp.zeros((sz.rows, sz.lanes), jnp.float32)
    sums = lax.fori_loop(0, N // 2, products, (zero,) * len(pairs), unroll=4)
    wide = -(-len(pairs) // 8) * 8
    rows = [jnp.sum(s, axis=0, keepdims=True) for s in sums]
    rows = jnp.concatenate(rows + [jnp.zeros((wide - len(rows), sz.lanes), jnp.float32)], axis=0)
    total = jnp.broadcast_to(jnp.sum(rows, axis=1, keepdims=True), rows.shape)
    line = jnp.sum(jnp.where(sub_iota(rows.shape) == lane_iota(rows.shape), total, 0.0), axis=0, keepdims=True)
    gram_out[...] = jnp.broadcast_to(line[None], gram_out.shape)


def combine_kernel(sz, gram_ref, u_ref, rho_ref, out_ref, scr):
    line = jnp.sum(gram_ref[...], axis=0)
    lane = lane_iota(line.shape)

    def entry(j, k):
        picked = jnp.where(lane == j * ITERS + k, line, 0.0)
        return jnp.broadcast_to(jnp.sum(picked, axis=1, keepdims=True), line.shape)

    g = [[entry(j, k) for k in range(ITERS)] for j in range(ITERS + 1)]
    zero = jnp.zeros_like(line)
    one = jnp.ones_like(line)

    def form(left, right, matrix):
        total = zero
        for j, a in enumerate(left):
            for k, b in enumerate(right):
                total = total + a * b * matrix(j, k)
        return total

    res = [one]
    direction = [one]
    sol = [zero] * ITERS
    product = g[0][0]
    for i in range(ITERS):
        alpha = product / form(direction, direction, lambda j, k: g[k][j] - g[k + 1][j])
        for k, b in enumerate(direction):
            sol[k] = sol[k] + alpha * b
        res = res + [zero]
        for k, b in enumerate(direction):
            res[k] = res[k] - alpha * b
            res[k + 1] = res[k + 1] + alpha * b
        if i + 1 < ITERS:
            following = form(res, res, lambda j, k: g[j][k])
            beta = following / product
            direction = [a + beta * b for a, b in zip(res, direction + [zero])]
            product = following

    below = lane_iota((1, sz.rows, sz.lanes)) < sz.width
    for a, (ref, weights) in enumerate(((u_ref, sol), (rho_ref, res))):

        def body(q, n):
            left, right = (sum(w * ref[k, pl.ds(q, n), i] for k, w in enumerate(weights)) for i in (0, 1))
            under = swap_blocks(jnp.where(below, left, roll(right, sz.width, 2)), sz.gy, sz.yl)
            over = swap_blocks(jnp.where(below, roll(left, sz.width, 2), right), sz.gy, sz.yl)
            for i in range(n):
                for p, v in ((q + i, under), (sz.planes - 1 - q - i, over)):
                    row = p * sz.group if isinstance(p, int) else pl.multiple_of(p * sz.group, 8)
                    scr[pl.ds(row, sz.group), :] = v[i]

        chunked(0, sz.planes // 2, sz.chunk // 2, body)
        for dest in range(sz.group):
            out_ref[dest, a] = scr[pl.ds(dest, sz.planes, stride=sz.group), :]


def unpack_kernel(sz, in_ref, sol_ref, res_ref):
    for a, out in ((0, sol_ref), (1, res_ref)):
        for c in range(sz.comps):
            halves = [in_ref[part_of(sz, half) * sz.gy + c, a] for half in range(sz.gx)]
            turned = jnp.concatenate(halves, axis=0).T
            for i, x in enumerate(x_order(sz)):
                out[c, x] = turned[i * sz.yl : (i + 1) * sz.yl]


def call(kernel, sz, ins, outs, scratch=(), name=None, sems=0, alias={}):
    outs = [jax.ShapeDtypeStruct(s, jnp.float32) for s in outs]
    own = [a.shape for i, a in enumerate(ins) if i not in alias]
    held = sum(math.prod(s) for s in own + [o.shape for o in outs] + list(scratch))
    scratch = [pltpu.VMEM(s, jnp.float32) for s in scratch]
    return pl.pallas_call(
        functools.partial(kernel, sz),
        in_specs=[pl.BlockSpec(memory_space=pltpu.HBM if sems else pltpu.VMEM)] * len(ins),
        out_specs=[pl.BlockSpec(memory_space=pltpu.VMEM)] * len(outs),
        out_shape=outs,
        scratch_shapes=scratch + ([pltpu.SemaphoreType.DMA((sems,))] if sems else []),
        compiler_params=pltpu.CompilerParams(vmem_limit_bytes=4 * held + 3 * 2**20),
        input_output_aliases=alias,
        name=name,
    )(*ins)


def shards(mesh, forcing, viscosity):
    comps, xl, yl, zl = forcing.shape
    sz = Sizes(mesh, comps, xl, yl, zl)
    N, W = sz.planes, sz.window
    plane = (sz.rows, sz.lanes)
    group_shape = (sz.group, 2, N, sz.lanes)
    arrays = [pltpu.with_memory_space_constraint(a, pltpu.HBM) for a in (forcing, viscosity)]
    (packed,) = call(
        pack_kernel, sz, arrays, [group_shape], [a.shape for a in arrays], name="pack", sems=1 + sz.comps
    )
    packed = lax.all_to_all(packed, ("gx", "gy"), 0, 0)
    edge_shapes = [(2, c) + plane for c in sz.hops if c < N for _ in range(2)]
    main, *edges = call(
        planes_kernel, sz, [packed], [(2, N) + plane] + edge_shapes, [(N * sz.group, sz.lanes)], name="planes"
    )
    halos = []
    if sz.paired:
        halos = [swapped_pairs(edge, sz, first) for first, edge in reversed(list(enumerate(edges)))][::-1]
    for j, count in enumerate([] if sz.paired else sz.hops):
        first, last = (edges.pop(0), edges.pop(0)) if count < N else (main, main)
        halos += [shifted(last, sz, j + 1), shifted(first, sz, -(j + 1))]
    devices = sz.group * sz.gz
    own = (N // 2, 2) + plane
    state = [(FINE_ARRAYS, W // 2 + 1, 2) + plane, (COARSE_ARRAYS, W // 4 + 1) + plane]
    results = [(ITERS,) + own, (ITERS + 1,) + own, (devices, 1, sz.lanes)]
    if sum(math.prod(shape) for shape in state) <= STATE_LIMIT:
        held = call(functools.partial(basis_kernel, 0), sz, [main], state, name="inner")
        ins = halos + list(held)
        alias = {len(halos): 0, len(halos) + 1: 1}
        *_, u, rho, gram = call(functools.partial(basis_kernel, 1), sz, ins, state + results, name="outer", alias=alias)
    else:
        u, rho, gram = call(functools.partial(basis_kernel, None), sz, [main] + halos, results, state, name="basis")
    gram = lax.all_to_all(gram, ("gx", "gy", "gz"), 0, 0)
    (mixed,) = call(
        combine_kernel, sz, [gram, u, rho], [group_shape], [(N * sz.group, sz.lanes)], name="combine"
    )
    mixed = lax.all_to_all(mixed, ("gx", "gy"), 0, 0)
    return tuple(call(unpack_kernel, sz, [mixed], [forcing.shape, forcing.shape], name="unpack"))


def solution(mesh):
    spec = P(None, "gx", "gy", "gz")
    return jax.shard_map(
        functools.partial(shards, dict(mesh.shape)),
        mesh=mesh,
        in_specs=(spec, P("gx", "gy", "gz")),
        out_specs=(spec, spec),
        check_vma=False,
    )
```

time: 72 us -> 66.6 us (0.925)
  waiting for transfers between devices: 6.79 us -> 2.92 us
  starting transfers between devices: 3.77 us -> 1.29 us
  local copies, waits for them, and re-layouts: 1.76 us -> 0 us
  blocking collectives: 49.5 us -> 51 us
  Pallas kernels: 9.19 us -> 10.4 us
    ppermute x2, waiting for transfers between devices: 6.79 us -> 2.92 us  [to_slab(): return lax.ppermute(x, ('gx', 'gz'), perm)]
    ppermute x2, starting transfers between devices: 3.77 us -> 1.29 us  [to_slab(): return lax.ppermute(x, ('gx', 'gz'), perm)]
    unnamed x4 -> x0, local copies, waits for them, and re-layouts: 1.76 us -> none
    all_to_all x1, blocking collectives: 8.88 us -> 10.4 us  [shards(): gram = lax.all_to_all(gram, ('gx', 'gy', 'gz'), 0, 0)]
    pallas_call x5 -> x6, Pallas kernels: 9.19 us -> 10.4 us  [call(): pl.pallas_call(functools.partial(kernel, sz), in_specs=[pl.BlockSpec(memo...]
  transfers between devices with their start and end apart: 2 -> 2, of which waited for: 2 -> 1; matrix products, arithmetic and copies ran while one was open for 0% -> 0% of each run, Pallas kernels for 0% -> 4%
where the time goes in v3:
time: 66.6 us; the launch traced here: 66.3 us
  blocking collectives  51 us (77%)
  Pallas kernels  10.4 us (16%)
  waiting for transfers between devices  2.92 us (4%)
  starting transfers between devices  1.29 us (2%)
    all_to_all x1, blocking collectives, shards(): packed = lax.all_to_all(packed, ('gx', 'gy'), 0, 0)  22.5 us
    all_to_all x1, blocking collectives, shards(): mixed = lax.all_to_all(mixed, ('gx', 'gy'), 0, 0)  18.1 us
    pallas_call x6, Pallas kernels, call(): pl.pallas_call(functools.partial(kernel, sz), in_specs=[pl.BlockSpec(memo...  10.4 us
    all_to_all x1, blocking collectives, shards(): gram = lax.all_to_all(gram, ('gx', 'gy', 'gz'), 0, 0)  10.4 us
    ppermute x2, waiting for transfers between devices, to_slab(): return lax.ppermute(x, ('gx', 'gz'), perm)  2.92 us
  transfers between devices with their start and end apart: 2, of which 1 were waited for; matrix products, arithmetic and copies ran while one was open for 0% of the time, Pallas kernels for 4%

profile of v3, /device:TPU:0, one launch (start us, length us, event | category | flops | bytes accessed | tf_op | source)
XLA Modules:
  0.0 66.3 jit_solution(7725794807880633151)
XLA Ops:
  0.6 1.3 %pack.1 = f32[8,2,64,128]{3,2,1,0:T(8,128)S(1)} custom-call(f32[3,8,16,128]{3,2,1,0:T(8,128)} %f_hbm.1, f32[8,16,128]{2,1,0:T(8,128)} %v_hbm.1), custom_call_target="tpu_custom_call" | custom-call | tf_op jit(solution)/shard_map/pack/pallas_call | solution.py:500
  1.9 22.5 %all_to_all.15.in_ref = f32[8,2,64,128]{3,2,1,0:T(8,128)S(1)} all-to-all(f32[8,2,64,128]{3,2,1,0:T(8,128)S(1)} %pack.1), channel_id=1, replica_groups=mesh['gx'=2,'gy'=4,'gz'=4] {'gx','gy'}, dimensions={0} | all-to-all | bytes 1048576 | tf_op jit(solution)/shard_map/all_to_all | solution.py:522
  24.4 0.7 %planes.1 = (f32[2,64,8,128]{3,2,1,0:T(8,128)S(1)}, f32[2,30,8,128]{3,2,1,0:T(8,128)S(1)}, f32[2,30,8,128]{3,2,1,0:T(8,128)S(1)}) custom-call(f32[8,2,64,128]{3,2,1,0:T(8,128)S(1)} %all_to_all.15.in_ref), custom_call_target="tpu_custom_call" | custom-call | tf_op jit(solution)/shard_map/planes/pallas_call | solution.py:500
  25.1 0.6 collective-permute-start
  25.7 0.7 %collective-permute-start.1 = (f32[2,30,8,128]{3,2,1,0:T(8,128)S(1)}, f32[2,30,8,128]{3,2,1,0:T(8,128)S(1)}, u32[]{:S(2)}, u32[]{:S(2)}) collective-permute-start(f32[2,30,8,128]{3,2,1,0:T(8,128)S(1)} %get-tuple-element.11), channel_id=1, source_target_pairs={{16,17},{17,16},{1,2},{2,1},{18,19},{19,18},{20,21},{21,20},{5,6},... | collective-permute-start | bytes 737288 | tf_op jit(solution)/shard_map/ppermute | solution.py:89
  26.4 2.4 %inner.1 = (f32[27,63,2,8,128]{4,3,2,1,0:T(8,128)S(1)}, f32[21,32,8,128]{3,2,1,0:T(8,128)S(1)}) custom-call(f32[2,64,8,128]{3,2,1,0:T(8,128)S(1)} %get-tuple-element.12.refs_0_), custom_call_target="tpu_custom_call" | custom-call | tf_op jit(solution)/shard_map/inner/pallas_call | solution.py:500
  28.8 2.9 %collective-permute-done.refs_0_ = f32[2,30,8,128]{3,2,1,0:T(8,128)S(1)} collective-permute-done((f32[2,30,8,128]{3,2,1,0:T(8,128)S(1)}, f32[2,30,8,128]{3,2,1,0:T(8,128)S(1)}, u32[]{:S(2)}, u32[]{:S(2)}) %collective-permute-start) | collective-permute-done | bytes 245792 | tf_op jit(solution)/shard_map/ppermute | solution.py:89
  31.7 0.0 collective-permute-done.1.refs_1_
  31.7 4.0 %outer.1 = (f32[27,63,2,8,128]{4,3,2,1,0:T(8,128)S(1)}, f32[21,32,8,128]{3,2,1,0:T(8,128)S(1)}, f32[3,32,2,8,128]{4,3,2,1,0:T(8,128)S(1)}, f32[4,32,2,8,128]{4,3,2,1,0:T(8,128)S(1)}, f32[32,1,128]{2,1,0:T(1,128)S(1)}) custom-call(f32[2,30,8,128]{3,2,1,0:T(8,128)S(1)} %collective-permute-done.refs_0_, ...), custom_call_target="tpu_custom_call", output_to_operand_aliasing={{0}: (2, {}), {1}: (3, {})} | custom-call | tf_op jit(solution)/shard_map/outer/pallas_call | solution.py:500
  35.8 10.4 %all_to_all.16.gram_ref = f32[32,1,128]{2,1,0:T(1,128)S(1)} all-to-all(f32[32,1,128]{2,1,0:T(1,128)S(1)} %get-tuple-element.15), channel_id=1, replica_groups=mesh['gx'=2,'gy'=4,'gz'=4] {'gx','gy','gz'}, dimensions={0} | all-to-all | bytes 32768 | tf_op jit(solution)/shard_map/all_to_all | solution.py:544
  46.2 1.1 %combine.1 = f32[8,2,64,128]{3,2,1,0:T(8,128)S(1)} custom-call(f32[32,1,128]{2,1,0:T(1,128)S(1)} %all_to_all.16.gram_ref, f32[3,32,2,8,128]{4,3,2,1,0:T(8,128)S(1)} %get-tuple-element.16.u_ref, f32[4,32,2,8,128]{4,3,2,1,0:T(8,128)S(1)} %get-tuple-element.17.rho_ref), custom_call_target="tpu_custom_call" | custom-call | tf_op jit(solution)/shard_map/combine/pallas_call | solution.py:500
  47.3 18.1 %all_to_all.17.in_ref = f32[8,2,64,128]{3,2,1,0:T(8,128)S(1)} all-to-all(f32[8,2,64,128]{3,2,1,0:T(8,128)S(1)} %combine.1), channel_id=1, replica_groups=mesh['gx'=2,'gy'=4,'gz'=4] {'gx','gy'}, dimensions={0} | all-to-all | bytes 1048576 | tf_op jit(solution)/shard_map/all_to_all | solution.py:548
  65.4 0.9 %unpack.1 = (f32[3,8,16,128]{3,2,1,0:T(8,128)}, f32[3,8,16,128]{3,2,1,0:T(8,128)}) custom-call(f32[8,2,64,128]{3,2,1,0:T(8,128)S(1)} %all_to_all.17.in_ref), custom_call_target="tpu_custom_call" | custom-call | tf_op jit(solution)/shard_map/unpack/pallas_call | solution.py:500
Async XLA Ops:
  25.1 6.6 %collective-permute-start = (f32[2,30,8,128]{3,2,1,0:T(8,128)S(1)}, f32[2,30,8,128]{3,2,1,0:T(8,128)S(1)}, u32[]{:S(2)}, u32[]{:S(2)}) collective-permute-start(f32[2,30,8,128]{3,2,1,0:T(8,128)S(1)} %get-tuple-element.10), channel_id=1, source_target_pairs={{0,16},{16,0},{17,1},{1,17},{2,18},{18,2},{19,3},{3,19},{4,20},{20... | collective-permute-start | bytes 737288 | tf_op jit(solution)/shard_map/ppermute | solution.py:89
  25.7 6.0 %collective-permute-start.1 = (f32[2,30,8,128]{3,2,1,0:T(8,128)S(1)}, f32[2,30,8,128]{3,2,1,0:T(8,128)S(1)}, u32[]{:S(2)}, u32[]{:S(2)}) collective-permute-start(f32[2,30,8,128]{3,2,1,0:T(8,128)S(1)} %get-tuple-element.11), channel_id=1, source_target_pairs={{16,17},{17,16},{1,2},{2,1},{18,19},{19,18},{20,21},{21,20},{5,6},... | collective-permute-start | bytes 737288 | tf_op jit(solution)/shard_map/ppermute | solution.py:89

commit v4 on v3

--- a/solution.py
+++ b/solution.py
@@ -14,7 +14,9 @@
 
 STEP = 2 * (CSWEEPS - 1) + 4
 HALO = ITERS * STEP
+MOMENTS = 2 * ITERS - 1
 BLOCK_ROWS = 1024
+GROUP = ("gy", "gx")
 STATE_LIMIT = 6 * 2**20
 
 
@@ -43,6 +45,56 @@
         v = jnp.where(low == high, v, jnp.where(low, from_left, from_right))
         step *= 2
     return v
+
+
+def two_sum(a, b):
+    s = a + b
+    t = s - a
+    return s, (a - (s - t)) + (b - t)
+
+
+class Pair:
+    def __init__(self, hi, lo):
+        self.hi, self.lo = hi, lo
+
+    @staticmethod
+    def of(hi, lo):
+        s = hi + lo
+        return Pair(s, lo - (s - hi))
+
+    def __add__(self, other):
+        s, e = two_sum(self.hi, other.hi)
+        return Pair.of(s, e + (self.lo + other.lo))
+
+    def __neg__(self):
+        return Pair(-self.hi, -self.lo)
+
+    def __sub__(self, other):
+        return self + -other
+
+    def twice(self):
+        return Pair(2.0 * self.hi, 2.0 * self.lo)
+
+    def __mul__(self, other):
+        p = self.hi * other.hi
+        (a, b), (c, d) = split(self.hi), split(other.hi)
+        e = ((a * c - p) + a * d + b * c) + b * d
+        return Pair.of(p, e + (self.hi * other.lo + self.lo * other.hi))
+
+    def __truediv__(self, other):
+        q = self.hi / other.hi
+        rest = self - other * Pair(q, jnp.zeros_like(q))
+        return Pair.of(q, rest.hi / other.hi)
+
+
+def split(a):
+    t = 4097.0 * a
+    hi = t - (t - a)
+    return hi, a - hi
+
+
+def total(terms):
+    return functools.reduce(lambda a, b: a + b, terms)
 
 
 def chunked(lo, hi, n, body):
@@ -108,6 +160,14 @@
     return list(range(0, sz.xl, 2)) + list(range(1, sz.xl, 2))
 
 
+def member_of(sz, x, y):
+    return y * sz.gx + x if GROUP[0] == "gy" else x * sz.gy + y
+
+
+def row_of(sz, member):
+    return member % sz.gx * sz.gy + member // sz.gx if GROUP[0] == "gy" else member
+
+
 def part_of(sz, half):
     odd = lax.axis_index("gz") % 2
     return jnp.where(odd == 1, sz.gx - 1 - half, half)
@@ -124,7 +184,7 @@
 
     def put(c, a, field):
         for half in range(sz.gx):
-            out_ref[part_of(sz, half) * sz.gy + c, a] = field[half * sz.planes : (half + 1) * sz.planes]
+            out_ref[member_of(sz, part_of(sz, half), c), a] = field[half * sz.planes : (half + 1) * sz.planes]
 
     for c in range(sz.comps, sz.gy):
         for a in range(2):
@@ -142,7 +202,7 @@
     edges, scr = rest[:-1], rest[-1]
     for a in range(2):
         for src in range(sz.group):
-            scr[pl.ds(src, sz.planes, stride=sz.group), :] = in_ref[src, a]
+            scr[pl.ds(row_of(sz, src), sz.planes, stride=sz.group), :] = in_ref[src, a]
 
         def body(p, n):
             rows = pl.multiple_of(p * sz.group, 8)
@@ -175,14 +235,15 @@
         next(it), next(it)
     if phase == 1 or phase == 0:
         fine_state, coarse_state = next(it), next(it)
-    u_out, rho_out, gram_out = (next(it) for _ in range(3)) if phase != 0 else (None,) * 3
     if phase is None:
         fine_state, coarse_state = next(it), next(it)
+    gram_out = next(it) if phase != 0 else None
     it = iter([fine_state.at[i] for i in range(FINE_ARRAYS)])
+    us = [next(it) for _ in range(ITERS)]
+    rhos = [next(it) for _ in range(ITERS + 1)]
     half, cin, cout, cyp, cym, cz, mass, od = (next(it) for _ in range(8))
     sin, sout, syp, sym, szp, szm = (next(it) for _ in range(6))
-    sms, sm2s, us = ([next(it) for _ in range(ITERS)] for _ in range(3))
-    rhos = [next(it) for _ in range(ITERS + 1)]
+    sms, sm2s = ([next(it) for _ in range(ITERS)] for _ in range(2))
     it = iter([coarse_state.at[i] for i in range(COARSE_ARRAYS)])
     twice, ccz, cod, kxp, kxm, kyp, kym, kzp, kzm = (next(it) for _ in range(9))
     corrections = [[next(it) for _ in range(CSWEEPS)] for _ in range(ITERS)]
@@ -400,77 +461,100 @@
             at = pl.ds(q, n)
             for i, image in enumerate(fine_apply(u, q, n)):
                 rho_next[at, i] = rho[at, i] - image
-
+                image_of[at, i] = image
+
+        image_of = sm2
         outer, known = outer + 1, known + 1
         run(outer, known, Q, C // 2, descend)
 
     if phase == 0:
         return
-    pairs = [(j, k) for j in range(ITERS + 1) for k in range(ITERS)]
-
-    def products(q, sums):
-        for i in (0, 1):
-            rv = [r[H + q, i] for r in rhos]
-            uv = [u[H + q, i] for u in us]
-            for k in range(ITERS):
-                u_out[k, q, i] = uv[k]
-            for j in range(ITERS + 1):
-                rho_out[j, q, i] = rv[j]
-            sums = tuple(s + rv[j] * uv[k] for s, (j, k) in zip(sums, pairs))
-        return sums
-
+    orders = [((n + 1) // 2, n // 2) for n in range(MOMENTS)]
     zero = jnp.zeros((sz.rows, sz.lanes), jnp.float32)
-    sums = lax.fori_loop(0, N // 2, products, (zero,) * len(pairs), unroll=4)
-    wide = -(-len(pairs) // 8) * 8
-    rows = [jnp.sum(s, axis=0, keepdims=True) for s in sums]
-    rows = jnp.concatenate(rows + [jnp.zeros((wide - len(rows), sz.lanes), jnp.float32)], axis=0)
-    total = jnp.broadcast_to(jnp.sum(rows, axis=1, keepdims=True), rows.shape)
-    line = jnp.sum(jnp.where(sub_iota(rows.shape) == lane_iota(rows.shape), total, 0.0), axis=0, keepdims=True)
+    sums = [(zero, zero)] * (2 * MOMENTS)
+    for q in range(H, Q):
+        rv, yv, uv = ([[ref[q, i] for i in (0, 1)] for ref in refs] for refs in (rhos[:ITERS], sm2s, us))
+        for place, left in enumerate((rv, yv)):
+            for n, (j, k) in enumerate(orders):
+                hi, lo = sums[place * MOMENTS + n]
+                hi, error = two_sum(hi, left[j][0] * uv[k][0] + left[j][1] * uv[k][1])
+                sums[place * MOMENTS + n] = (hi, lo + error)
+    wide = -(-len(sums) // 8) * 8
+
+    def rows_of(values, fold):
+        rows = [fold(v, axis=0, keepdims=True) for v in values]
+        return jnp.concatenate(rows + [jnp.zeros((wide - len(rows), sz.lanes), jnp.float32)], axis=0)
+
+    most = jnp.max(rows_of([jnp.abs(hi) for hi, _ in sums], jnp.max), axis=1, keepdims=True)
+    grid = float(sz.rows * sz.lanes) * jnp.broadcast_to(most, (wide, sz.lanes))
+    coarse = [(hi + grid[n : n + 1]) - grid[n : n + 1] for n, (hi, _) in enumerate(sums)]
+    rest = [(hi - c) + lo for c, (hi, lo) in zip(coarse, sums)]
+    line = jnp.zeros((1, sz.lanes), jnp.float32)
+    for offset, values in ((0, coarse), (wide, rest)):
+        rows = rows_of(values, jnp.sum)
+        each = jnp.broadcast_to(jnp.sum(rows, axis=1, keepdims=True), rows.shape)
+        here = sub_iota(rows.shape) + offset == lane_iota(rows.shape)
+        line = line + jnp.sum(jnp.where(here, each, 0.0), axis=0, keepdims=True)
     gram_out[...] = jnp.broadcast_to(line[None], gram_out.shape)
 
 
-def combine_kernel(sz, gram_ref, u_ref, rho_ref, out_ref, scr):
-    line = jnp.sum(gram_ref[...], axis=0)
-    lane = lane_iota(line.shape)
-
-    def entry(j, k):
-        picked = jnp.where(lane == j * ITERS + k, line, 0.0)
-        return jnp.broadcast_to(jnp.sum(picked, axis=1, keepdims=True), line.shape)
-
-    g = [[entry(j, k) for k in range(ITERS)] for j in range(ITERS + 1)]
-    zero = jnp.zeros_like(line)
-    one = jnp.ones_like(line)
-
-    def form(left, right, matrix):
-        total = zero
-        for j, a in enumerate(left):
-            for k, b in enumerate(right):
-                total = total + a * b * matrix(j, k)
-        return total
-
-    res = [one]
-    direction = [one]
-    sol = [zero] * ITERS
-    product = g[0][0]
+def combine_kernel(sz, gram_ref, fine_ref, out_ref, scr):
+    parts = gram_ref[:, 0, :]
+    wide = -(-2 * MOMENTS // 8) * 8
+    hi, lo = parts, roll(parts, -wide, 1)
+    while hi.shape[0] % 16 == 0:
+        n = hi.shape[0] // 2
+        hi, error = two_sum(hi[:n], hi[n:])
+        lo = lo[:n] + lo[n:] + error
+    sum_hi, sum_lo = hi[:1], lo[:1]
+    for i in range(1, hi.shape[0]):
+        sum_hi, error = two_sum(sum_hi, hi[i : i + 1])
+        sum_lo = sum_lo + (lo[i : i + 1] + error)
+    lane = lane_iota(sum_hi.shape)
+
+    def entry(n):
+        halves = []
+        for v in (sum_hi, sum_lo):
+            picked = jnp.sum(jnp.where(lane == n, v, 0.0), axis=1, keepdims=True)
+            halves.append(jnp.broadcast_to(picked, v.shape))
+        return Pair.of(*halves)
+
+    moments = [entry(n) for n in range(2 * MOMENTS)]
+
+    def form(v, moments):
+        terms = []
+        for n in range(2 * len(v) - 1):
+            pairs = [(j, n - j) for j in range(len(v)) if j <= n - j < len(v)]
+            weight = total([v[j] * v[k] if j == k else (v[j] * v[k]).twice() for j, k in pairs])
+            terms.append(weight * moments[n])
+        return total(terms)
+
+    zero = Pair(jnp.zeros_like(sum_hi), jnp.zeros_like(sum_hi))
+    one = Pair(jnp.ones_like(sum_hi), jnp.zeros_like(sum_hi))
+    res, direction, sol = [one], [one], []
+    product = moments[0]
     for i in range(ITERS):
-        alpha = product / form(direction, direction, lambda j, k: g[k][j] - g[k + 1][j])
-        for k, b in enumerate(direction):
-            sol[k] = sol[k] + alpha * b
-        res = res + [zero]
-        for k, b in enumerate(direction):
-            res[k] = res[k] - alpha * b
-            res[k + 1] = res[k + 1] + alpha * b
+        image = form(direction, moments[MOMENTS:]) if i else moments[MOMENTS]
+        alpha = product / image
+        steps = [alpha * b for b in direction] if i else [alpha]
+        sol = [s + t for s, t in zip(sol, steps)] + steps[-1:]
+        res = [r - t for r, t in zip(res, steps)] + [zero]
+        res = res[:1] + [r + t for r, t in zip(res[1:-1], steps)] + steps[-1:]
         if i + 1 < ITERS:
-            following = form(res, res, lambda j, k: g[j][k])
+            following = form(res, moments)
             beta = following / product
-            direction = [a + beta * b for a, b in zip(res, direction + [zero])]
+            direction = [a + beta * b for a, b in zip(res, direction)] + res[-1:]
             product = following
 
+    sol = [s.hi.reshape(1, 1, sz.lanes) for s in sol]
+    res = [s.hi.reshape(1, 1, sz.lanes) for s in res]
     below = lane_iota((1, sz.rows, sz.lanes)) < sz.width
-    for a, (ref, weights) in enumerate(((u_ref, sol), (rho_ref, res))):
+    for a, (first, weights) in enumerate(((0, sol), (ITERS, res))):
 
         def body(q, n):
-            left, right = (sum(w * ref[k, pl.ds(q, n), i] for k, w in enumerate(weights)) for i in (0, 1))
+            left, right = (
+                sum(w * fine_ref[first + k, pl.ds(HALO + q, n), i] for k, w in enumerate(weights)) for i in (0, 1)
+            )
             under = swap_blocks(jnp.where(below, left, roll(right, sz.width, 2)), sz.gy, sz.yl)
             over = swap_blocks(jnp.where(below, roll(left, sz.width, 2), right), sz.gy, sz.yl)
             for i in range(n):
@@ -480,13 +564,13 @@
 
         chunked(0, sz.planes // 2, sz.chunk // 2, body)
         for dest in range(sz.group):
-            out_ref[dest, a] = scr[pl.ds(dest, sz.planes, stride=sz.group), :]
+            out_ref[dest, a] = scr[pl.ds(row_of(sz, dest), sz.planes, stride=sz.group), :]
 
 
 def unpack_kernel(sz, in_ref, sol_ref, res_ref):
     for a, out in ((0, sol_ref), (1, res_ref)):
         for c in range(sz.comps):
-            halves = [in_ref[part_of(sz, half) * sz.gy + c, a] for half in range(sz.gx)]
+            halves = [in_ref[member_of(sz, part_of(sz, half), c), a] for half in range(sz.gx)]
             turned = jnp.concatenate(halves, axis=0).T
             for i, x in enumerate(x_order(sz)):
                 out[c, x] = turned[i * sz.yl : (i + 1) * sz.yl]
@@ -519,7 +603,7 @@
     (packed,) = call(
         pack_kernel, sz, arrays, [group_shape], [a.shape for a in arrays], name="pack", sems=1 + sz.comps
     )
-    packed = lax.all_to_all(packed, ("gx", "gy"), 0, 0)
+    packed = lax.all_to_all(packed, GROUP, 0, 0)
     edge_shapes = [(2, c) + plane for c in sz.hops if c < N for _ in range(2)]
     main, *edges = call(
         planes_kernel, sz, [packed], [(2, N) + plane] + edge_shapes, [(N * sz.group, sz.lanes)], name="planes"
@@ -531,21 +615,21 @@
         first, last = (edges.pop(0), edges.pop(0)) if count < N else (main, main)
         halos += [shifted(last, sz, j + 1), shifted(first, sz, -(j + 1))]
     devices = sz.group * sz.gz
-    own = (N // 2, 2) + plane
     state = [(FINE_ARRAYS, W // 2 + 1, 2) + plane, (COARSE_ARRAYS, W // 4 + 1) + plane]
-    results = [(ITERS,) + own, (ITERS + 1,) + own, (devices, 1, sz.lanes)]
+    gram_shape = (devices, 1, sz.lanes)
     if sum(math.prod(shape) for shape in state) <= STATE_LIMIT:
         held = call(functools.partial(basis_kernel, 0), sz, [main], state, name="inner")
-        ins = halos + list(held)
         alias = {len(halos): 0, len(halos) + 1: 1}
-        *_, u, rho, gram = call(functools.partial(basis_kernel, 1), sz, ins, state + results, name="outer", alias=alias)
+        outer = functools.partial(basis_kernel, 1)
+        fine, _, gram = call(outer, sz, halos + list(held), state + [gram_shape], name="outer", alias=alias)
     else:
-        u, rho, gram = call(functools.partial(basis_kernel, None), sz, [main] + halos, results, state, name="basis")
+        whole = functools.partial(basis_kernel, None)
+        fine, _, gram = call(whole, sz, [main] + halos, state + [gram_shape], name="basis")
     gram = lax.all_to_all(gram, ("gx", "gy", "gz"), 0, 0)
     (mixed,) = call(
-        combine_kernel, sz, [gram, u, rho], [group_shape], [(N * sz.group, sz.lanes)], name="combine"
+        combine_kernel, sz, [gram, fine], [group_shape], [(N * sz.group, sz.lanes)], name="combine"
     )
-    mixed = lax.all_to_all(mixed, ("gx", "gy"), 0, 0)
+    mixed = lax.all_to_all(mixed, GROUP, 0, 0)
     return tuple(call(unpack_kernel, sz, [mixed], [forcing.shape, forcing.shape], name="unpack"))
 
 

time: 66.6 us -> 66.6 us (level)
  starting transfers between devices: 1.29 us -> 2.15 us
  waiting for transfers between devices: 2.92 us -> 2.09 us
    all_to_all x2, blocking collectives: 40.6 us -> 38.8 us  [the longest x1 21.6 us: shards(): packed = lax.all_to_all(packed, GROUP, 0, 0)]
    all_to_all x1, blocking collectives: 10.4 us -> 12.1 us  [shards(): gram = lax.all_to_all(gram, ('gx', 'gy', 'gz'), 0, 0)]
    ppermute x2, starting transfers between devices: 1.29 us -> 2.15 us  [to_slab(): return lax.ppermute(x, ('gx', 'gz'), perm)]
    ppermute x2, waiting for transfers between devices: 2.92 us -> 2.09 us  [to_slab(): return lax.ppermute(x, ('gx', 'gz'), perm)]
where the time goes in v4:
time: 66.6 us; the launch traced here: 66.3 us
  blocking collectives  50.9 us (76%)
  Pallas kernels  10.5 us (16%)
  starting transfers between devices  2.15 us (3%)
  waiting for transfers between devices  2.09 us (3%)
  between operations  0.67 us (1%)
    all_to_all x1, blocking collectives, shards(): packed = lax.all_to_all(packed, GROUP, 0, 0)  21.6 us
    all_to_all x1, blocking collectives, shards(): mixed = lax.all_to_all(mixed, GROUP, 0, 0)  17.2 us
    all_to_all x1, blocking collectives, shards(): gram = lax.all_to_all(gram, ('gx', 'gy', 'gz'), 0, 0)  12.1 us
    pallas_call x6, Pallas kernels, call(): pl.pallas_call(functools.partial(kernel, sz), in_specs=[pl.BlockSpec(memo...  10.5 us
    ppermute x2, starting transfers between devices, to_slab(): return lax.ppermute(x, ('gx', 'gz'), perm)  2.15 us
    ppermute x2, waiting for transfers between devices, to_slab(): return lax.ppermute(x, ('gx', 'gz'), perm)  2.09 us
  transfers between devices with their start and end apart: 2, of which 1 were waited for; matrix products, arithmetic and copies ran while one was open for 0% of the time, Pallas kernels for 4%

profile of v4, /device:TPU:0, one launch (start us, length us, event | category | flops | bytes accessed | tf_op | source)
XLA Modules:
  0.0 66.3 jit_solution(11650358319491621443)
XLA Ops:
  0.6 1.3 %pack.1 = f32[8,2,64,128]{3,2,1,0:T(8,128)S(1)} custom-call(f32[3,8,16,128]{3,2,1,0:T(8,128)} %f_hbm.1, f32[8,16,128]{2,1,0:T(8,128)} %v_hbm.1), custom_call_target="tpu_custom_call" | custom-call | tf_op jit(solution)/shard_map/pack/pallas_call | solution.py:584
  1.9 21.6 %all_to_all.15.in_ref = f32[8,2,64,128]{3,2,1,0:T(8,128)S(1)} all-to-all(f32[8,2,64,128]{3,2,1,0:T(8,128)S(1)} %pack.1), channel_id=1, replica_groups=mesh['gx'=2,'gy'=4,'gz'=4] {'gy','gx'}, dimensions={0} | all-to-all | bytes 1048576 | tf_op jit(solution)/shard_map/all_to_all | solution.py:606
  23.6 0.7 %planes.1 = (f32[2,64,8,128]{3,2,1,0:T(8,128)S(1)}, f32[2,30,8,128]{3,2,1,0:T(8,128)S(1)}, f32[2,30,8,128]{3,2,1,0:T(8,128)S(1)}) custom-call(f32[8,2,64,128]{3,2,1,0:T(8,128)S(1)} %all_to_all.15.in_ref), custom_call_target="tpu_custom_call" | custom-call | tf_op jit(solution)/shard_map/planes/pallas_call | solution.py:584
  24.3 1.5 %collective-permute-start = (f32[2,30,8,128]{3,2,1,0:T(8,128)S(1)}, f32[2,30,8,128]{3,2,1,0:T(8,128)S(1)}, u32[]{:S(2)}, u32[]{:S(2)}) collective-permute-start(f32[2,30,8,128]{3,2,1,0:T(8,128)S(1)} %get-tuple-element.9), channel_id=1, source_target_pairs={{0,16},{16,0},{17,1},{1,17},{2,18},{18,2},{19,3},{3,19},{4,20},{20... | collective-permute-start | bytes 737288 | tf_op jit(solution)/shard_map/ppermute | solution.py:141
  25.7 0.7 %collective-permute-start.1 = (f32[2,30,8,128]{3,2,1,0:T(8,128)S(1)}, f32[2,30,8,128]{3,2,1,0:T(8,128)S(1)}, u32[]{:S(2)}, u32[]{:S(2)}) collective-permute-start(f32[2,30,8,128]{3,2,1,0:T(8,128)S(1)} %get-tuple-element.10), channel_id=1, source_target_pairs={{16,17},{17,16},{1,2},{2,1},{18,19},{19,18},{20,21},{21,20},{5,6},... | collective-permute-start | bytes 737288 | tf_op jit(solution)/shard_map/ppermute | solution.py:141
  26.4 2.4 %inner.1 = (f32[27,63,2,8,128]{4,3,2,1,0:T(8,128)S(1)}, f32[21,32,8,128]{3,2,1,0:T(8,128)S(1)}) custom-call(f32[2,64,8,128]{3,2,1,0:T(8,128)S(1)} %get-tuple-element.11.refs_0_), custom_call_target="tpu_custom_call" | custom-call | tf_op jit(solution)/shard_map/inner/pallas_call | solution.py:584
  28.8 2.1 %collective-permute-done.refs_0_ = f32[2,30,8,128]{3,2,1,0:T(8,128)S(1)} collective-permute-done((f32[2,30,8,128]{3,2,1,0:T(8,128)S(1)}, f32[2,30,8,128]{3,2,1,0:T(8,128)S(1)}, u32[]{:S(2)}, u32[]{:S(2)}) %collective-permute-start) | collective-permute-done | bytes 245792 | tf_op jit(solution)/shard_map/ppermute | solution.py:141
  30.9 0.0 collective-permute-done.1.refs_1_
  30.9 3.9 %outer.1 = (f32[27,63,2,8,128]{4,3,2,1,0:T(8,128)S(1)}, f32[21,32,8,128]{3,2,1,0:T(8,128)S(1)}, f32[32,1,128]{2,1,0:T(1,128)S(1)}) custom-call(f32[2,30,8,128]{3,2,1,0:T(8,128)S(1)} %collective-permute-done.refs_0_, f32[2,30,8,128]{3,2,1,0:T(8,128)S(1)} %collective-permute-done.1.refs_1_, ...), custom_call_target="tpu_custom_call", output_to_operand_aliasing={{0}: (2, {}), {1}: (3, {})} | custom-call | tf_op jit(solution)/shard_map/outer/pallas_call | solution.py:584
  34.8 12.1 %all_to_all.16.gram_ref = f32[32,1,128]{2,1,0:T(1,128)S(1)} all-to-all(f32[32,1,128]{2,1,0:T(1,128)S(1)} %get-tuple-element.14), channel_id=1, replica_groups=mesh['gx'=2,'gy'=4,'gz'=4] {'gx','gy','gz'}, dimensions={0} | all-to-all | bytes 32768 | tf_op jit(solution)/shard_map/all_to_all | solution.py:628
  46.8 1.4 %combine.1 = f32[8,2,64,128]{3,2,1,0:T(8,128)S(1)} custom-call(f32[32,1,128]{2,1,0:T(1,128)S(1)} %all_to_all.16.gram_ref, f32[27,63,2,8,128]{4,3,2,1,0:T(8,128)S(1)} %get-tuple-element.15.fine_ref), custom_call_target="tpu_custom_call" | custom-call | tf_op jit(solution)/shard_map/combine/pallas_call | solution.py:584
  48.2 17.2 %all_to_all.17.in_ref = f32[8,2,64,128]{3,2,1,0:T(8,128)S(1)} all-to-all(f32[8,2,64,128]{3,2,1,0:T(8,128)S(1)} %combine.1), channel_id=1, replica_groups=mesh['gx'=2,'gy'=4,'gz'=4] {'gy','gx'}, dimensions={0} | all-to-all | bytes 1048576 | tf_op jit(solution)/shard_map/all_to_all | solution.py:632
  65.4 0.9 %unpack.1 = (f32[3,8,16,128]{3,2,1,0:T(8,128)}, f32[3,8,16,128]{3,2,1,0:T(8,128)}) custom-call(f32[8,2,64,128]{3,2,1,0:T(8,128)S(1)} %all_to_all.17.in_ref), custom_call_target="tpu_custom_call" | custom-call | tf_op jit(solution)/shard_map/unpack/pallas_call | solution.py:584
Async XLA Ops:
  24.3 6.6 %collective-permute-start = (f32[2,30,8,128]{3,2,1,0:T(8,128)S(1)}, f32[2,30,8,128]{3,2,1,0:T(8,128)S(1)}, u32[]{:S(2)}, u32[]{:S(2)}) collective-permute-start(f32[2,30,8,128]{3,2,1,0:T(8,128)S(1)} %get-tuple-element.9), channel_id=1, source_target_pairs={{0,16},{16,0},{17,1},{1,17},{2,18},{18,2},{19,3},{3,19},{4,20},{20... | collective-permute-start | bytes 737288 | tf_op jit(solution)/shard_map/ppermute | solution.py:141
  25.7 5.2 %collective-permute-start.1 = (f32[2,30,8,128]{3,2,1,0:T(8,128)S(1)}, f32[2,30,8,128]{3,2,1,0:T(8,128)S(1)}, u32[]{:S(2)}, u32[]{:S(2)}) collective-permute-start(f32[2,30,8,128]{3,2,1,0:T(8,128)S(1)} %get-tuple-element.10), channel_id=1, source_target_pairs={{16,17},{17,16},{1,2},{2,1},{18,19},{19,18},{20,21},{21,20},{5,6},... | collective-permute-start | bytes 737288 | tf_op jit(solution)/shard_map/ppermute | solution.py:141

commit v5 on v4

--- a/solution.py
+++ b/solution.py
@@ -33,16 +33,20 @@
     return pltpu.roll(v, shift % size, dim)
 
 
+def lane_xor(v, bit):
+    flat = v.reshape(-1, v.shape[-1])
+    return jnp.take_along_axis(flat, lane_iota(flat.shape) ^ bit, axis=1, mode="promise_in_bounds").reshape(v.shape)
+
+
 def swap_blocks(v, count, width):
     sub, lane = sub_iota(v.shape), lane_iota(v.shape)
     step = 1
     while step < count:
         low = (sub // step) % 2 == 1
         high = (lane // (step * width)) % 2 == 1
-        rows, lanes = v.ndim - 2, v.ndim - 1
-        from_left = roll(roll(v, step, rows), -step * width, lanes)
-        from_right = roll(roll(v, -step, rows), step * width, lanes)
-        v = jnp.where(low == high, v, jnp.where(low, from_left, from_right))
+        rows = v.ndim - 2
+        moved = lane_xor(v, step * width)
+        v = jnp.where(low == high, v, jnp.where(low, roll(moved, step, rows), roll(moved, -step, rows)))
         step *= 2
     return v
 
@@ -345,7 +349,7 @@
     def gather_block(fine, n):
         t = fine.reshape(n, 2, sz.rows, sz.lanes)
         t = t[:, 0] + t[:, 1]
-        return t + jnp.where(lane % 2 == 0, roll(t, -1, 2), roll(t, 1, 2))
+        return t + lane_xor(t, 1)
 
     def coarse_visc(q, n):
         fine = pl.ds(2 * q, 2 * n)

time: 66.6 us -> 66.2 us (level)
  no operation moved by 1% of the time
where the time goes in v5:
time: 66.2 us; the launch traced here: 65.9 us
  blocking collectives  50.9 us (77%)
  Pallas kernels  10.1 us (15%)
  starting transfers between devices  2.15 us (3%)
  waiting for transfers between devices  2.05 us (3%)
    all_to_all x1, blocking collectives, shards(): packed = lax.all_to_all(packed, GROUP, 0, 0)  21.6 us
    all_to_all x1, blocking collectives, shards(): mixed = lax.all_to_all(mixed, GROUP, 0, 0)  17.2 us
    all_to_all x1, blocking collectives, shards(): gram = lax.all_to_all(gram, ('gx', 'gy', 'gz'), 0, 0)  12.1 us
    pallas_call x6, Pallas kernels, call(): pl.pallas_call(functools.partial(kernel, sz), in_specs=[pl.BlockSpec(memo...  10.1 us
    ppermute x2, starting transfers between devices, to_slab(): return lax.ppermute(x, ('gx', 'gz'), perm)  2.15 us
    ppermute x2, waiting for transfers between devices, to_slab(): return lax.ppermute(x, ('gx', 'gz'), perm)  2.05 us
  transfers between devices with their start and end apart: 2, of which 1 were waited for; matrix products, arithmetic and copies ran while one was open for 0% of the time, Pallas kernels for 4%

profile of v5, /device:TPU:0, one launch (start us, length us, event | category | flops | bytes accessed | tf_op | source)
XLA Modules:
  0.0 65.9 jit_solution(10488679219333762615)
XLA Ops:
  0.6 1.3 %pack.1 = f32[8,2,64,128]{3,2,1,0:T(8,128)S(1)} custom-call(f32[3,8,16,128]{3,2,1,0:T(8,128)} %f_hbm.1, f32[8,16,128]{2,1,0:T(8,128)} %v_hbm.1), custom_call_target="tpu_custom_call" | custom-call | tf_op jit(solution)/shard_map/pack/pallas_call | solution.py:588
  1.9 21.6 %all_to_all.15.in_ref = f32[8,2,64,128]{3,2,1,0:T(8,128)S(1)} all-to-all(f32[8,2,64,128]{3,2,1,0:T(8,128)S(1)} %pack.1), channel_id=1, replica_groups=mesh['gx'=2,'gy'=4,'gz'=4] {'gy','gx'}, dimensions={0} | all-to-all | bytes 1048576 | tf_op jit(solution)/shard_map/all_to_all | solution.py:610
  23.6 0.5 planes.1
  24.0 1.5 %collective-permute-start = (f32[2,30,8,128]{3,2,1,0:T(8,128)S(1)}, f32[2,30,8,128]{3,2,1,0:T(8,128)S(1)}, u32[]{:S(2)}, u32[]{:S(2)}) collective-permute-start(f32[2,30,8,128]{3,2,1,0:T(8,128)S(1)} %get-tuple-element.9), channel_id=1, source_target_pairs={{0,16},{16,0},{17,1},{1,17},{2,18},{18,2},{19,3},{3,19},{4,20},{20... | collective-permute-start | bytes 737288 | tf_op jit(solution)/shard_map/ppermute | solution.py:145
  25.5 0.7 %collective-permute-start.1 = (f32[2,30,8,128]{3,2,1,0:T(8,128)S(1)}, f32[2,30,8,128]{3,2,1,0:T(8,128)S(1)}, u32[]{:S(2)}, u32[]{:S(2)}) collective-permute-start(f32[2,30,8,128]{3,2,1,0:T(8,128)S(1)} %get-tuple-element.10), channel_id=1, source_target_pairs={{16,17},{17,16},{1,2},{2,1},{18,19},{19,18},{20,21},{21,20},{5,6},... | collective-permute-start | bytes 737288 | tf_op jit(solution)/shard_map/ppermute | solution.py:145
  26.2 2.4 %inner.1 = (f32[27,63,2,8,128]{4,3,2,1,0:T(8,128)S(1)}, f32[21,32,8,128]{3,2,1,0:T(8,128)S(1)}) custom-call(f32[2,64,8,128]{3,2,1,0:T(8,128)S(1)} %get-tuple-element.11.refs_0_), custom_call_target="tpu_custom_call" | custom-call | tf_op jit(solution)/shard_map/inner/pallas_call | solution.py:588
  28.6 2.0 %collective-permute-done.refs_0_ = f32[2,30,8,128]{3,2,1,0:T(8,128)S(1)} collective-permute-done((f32[2,30,8,128]{3,2,1,0:T(8,128)S(1)}, f32[2,30,8,128]{3,2,1,0:T(8,128)S(1)}, u32[]{:S(2)}, u32[]{:S(2)}) %collective-permute-start) | collective-permute-done | bytes 245792 | tf_op jit(solution)/shard_map/ppermute | solution.py:145
  30.6 0.0 collective-permute-done.1.refs_1_
  30.6 3.9 %outer.1 = (f32[27,63,2,8,128]{4,3,2,1,0:T(8,128)S(1)}, f32[21,32,8,128]{3,2,1,0:T(8,128)S(1)}, f32[32,1,128]{2,1,0:T(1,128)S(1)}) custom-call(f32[2,30,8,128]{3,2,1,0:T(8,128)S(1)} %collective-permute-done.refs_0_, f32[2,30,8,128]{3,2,1,0:T(8,128)S(1)} %collective-permute-done.1.refs_1_, ...), custom_call_target="tpu_custom_call", output_to_operand_aliasing={{0}: (2, {}), {1}: (3, {})} | custom-call | tf_op jit(solution)/shard_map/outer/pallas_call | solution.py:588
  34.6 12.1 %all_to_all.16.gram_ref = f32[32,1,128]{2,1,0:T(1,128)S(1)} all-to-all(f32[32,1,128]{2,1,0:T(1,128)S(1)} %get-tuple-element.14), channel_id=1, replica_groups=mesh['gx'=2,'gy'=4,'gz'=4] {'gx','gy','gz'}, dimensions={0} | all-to-all | bytes 32768 | tf_op jit(solution)/shard_map/all_to_all | solution.py:632
  46.7 1.1 %combine.1 = f32[8,2,64,128]{3,2,1,0:T(8,128)S(1)} custom-call(f32[32,1,128]{2,1,0:T(1,128)S(1)} %all_to_all.16.gram_ref, f32[27,63,2,8,128]{4,3,2,1,0:T(8,128)S(1)} %get-tuple-element.15.fine_ref), custom_call_target="tpu_custom_call" | custom-call | tf_op jit(solution)/shard_map/combine/pallas_call | solution.py:588
  47.8 17.2 %all_to_all.17.in_ref = f32[8,2,64,128]{3,2,1,0:T(8,128)S(1)} all-to-all(f32[8,2,64,128]{3,2,1,0:T(8,128)S(1)} %combine.1), channel_id=1, replica_groups=mesh['gx'=2,'gy'=4,'gz'=4] {'gy','gx'}, dimensions={0} | all-to-all | bytes 1048576 | tf_op jit(solution)/shard_map/all_to_all | solution.py:636
  65.0 0.9 %unpack.1 = (f32[3,8,16,128]{3,2,1,0:T(8,128)}, f32[3,8,16,128]{3,2,1,0:T(8,128)}) custom-call(f32[8,2,64,128]{3,2,1,0:T(8,128)S(1)} %all_to_all.17.in_ref), custom_call_target="tpu_custom_call" | custom-call | tf_op jit(solution)/shard_map/unpack/pallas_call | solution.py:588
Async XLA Ops:
  24.0 6.6 %collective-permute-start = (f32[2,30,8,128]{3,2,1,0:T(8,128)S(1)}, f32[2,30,8,128]{3,2,1,0:T(8,128)S(1)}, u32[]{:S(2)}, u32[]{:S(2)}) collective-permute-start(f32[2,30,8,128]{3,2,1,0:T(8,128)S(1)} %get-tuple-element.9), channel_id=1, source_target_pairs={{0,16},{16,0},{17,1},{1,17},{2,18},{18,2},{19,3},{3,19},{4,20},{20... | collective-permute-start | bytes 737288 | tf_op jit(solution)/shard_map/ppermute | solution.py:145
  25.5 5.2 %collective-permute-start.1 = (f32[2,30,8,128]{3,2,1,0:T(8,128)S(1)}, f32[2,30,8,128]{3,2,1,0:T(8,128)S(1)}, u32[]{:S(2)}, u32[]{:S(2)}) collective-permute-start(f32[2,30,8,128]{3,2,1,0:T(8,128)S(1)} %get-tuple-element.10), channel_id=1, source_target_pairs={{16,17},{17,16},{1,2},{2,1},{18,19},{19,18},{20,21},{21,20},{5,6},... | collective-permute-start | bytes 737288 | tf_op jit(solution)/shard_map/ppermute | solution.py:145
